TPU v7x, 256 devices: a whole 4x4x8 slice. The times are simulated.
256 devices in a mesh: group: 2 (over z_lo), dp: 32 (over y, z_hi, core), mp: 4 (over x).
Axes of the slice: x: 4, y: 4, z: 8 (z_hi: 4, z_lo: 2; z = z_hi * 2 + z_lo), core: 2. Of those that a mesh axis runs over, the one named last changes fastest.
Arguments:
- image_features: bfloat16 [8192, 6144], P('dp', 'mp'), may hold values from -6 to 6
- text_features: bfloat16 [8192, 1024], P('dp', 'mp'), may hold values from -6 to 6
- image_gain: float32 [6144], P('mp'), may hold values from 0.25 to 1.75
- text_gain: float32 [1024], P('mp'), may hold values from 0.25 to 1.75
- image_proj: bfloat16 [6144, 1024], P('mp'), may hold values from -1 to 1
- text_proj: bfloat16 [1024, 1024], P('mp'), may hold values from -1 to 1
- pair: int32 [8192], replicated, may hold values from 0 to 8191, each once
- logit_scale: float32 [], replicated, may hold values from 10 to 100
Outputs:
- embedding_grads: float32 [2, 8192, 1024], P('group', ('dp', 'mp'))
- loss: float32 [], replicated
Inputs may be any that keep to these rules, and one draw needn't show every extreme that they name: `pair`: each caption belongs to exactly one image.
All inputs are finite; a program needn't handle non-finite values.
Results may differ from a plain program's by a relative error of at most 0.0061.
Values may be sent and summed in bfloat16 or wider, within the bound.
A program may use at most 128 MiB of HBM per device.

v0:
```python
import functools

import jax
import jax.numpy as jnp
from jax import lax
from jax.sharding import Mesh
from jax.sharding import PartitionSpec as P

DP_MP = ("dp_0", "dp_1", "dp_2", "mp")
DP = ("dp_0", "dp_1", "dp_2")
GROUP_DP_MP = ("group", "dp_0", "dp_1", "dp_2", "mp")


epsilon = 1e-05


def from_everyone(shard, axis):
    peers = lax.axis_size(axis)
    return lax.all_to_all(
        jnp.broadcast_to(shard[None], (peers, *shard.shape)), axis, 0, 0, tiled=True
    )


def of_everyone(shard, axis):
    everything = from_everyone(shard, axis)
    return jnp.sum(everything, axis=0)


def together(arrays, axis):
    ends = [0]
    for a in arrays:
        ends.append(ends[-1] + a.size)
    so_far = of_everyone(jnp.concatenate([a.ravel() for a in arrays]), axis)
    return tuple((so_far[b:e].reshape(a.shape) for a, b, e in zip(arrays, ends, ends[1:])))


def in_blocks(shard, dim, peers):
    dims = shard.shape
    parts = shard.reshape(*dims[:dim], peers, dims[dim] // peers, *dims[dim + 1 :])
    return jnp.moveaxis(parts, dim, 0)


def sum_at_owner(shard, axis, dim):
    peers = lax.axis_size(axis)
    parts = lax.all_to_all(in_blocks(shard, dim, peers), axis, 0, 0, tiled=True)
    return jnp.sum(parts, axis=0)


def partner(shard, axis, distance):
    return lax.ppermute(shard, axis, [(i, i ^ 1 << distance) for i in range(lax.axis_size(axis))])


def laid_out(parts, dim):
    dims = list(parts.shape[1:])
    dims[dim] *= parts.shape[0]
    return jnp.moveaxis(parts, 0, dim).reshape(dims)


def all_blocks(shard, axes, turns):
    parts = shard[None]
    for k in turns:
        parts = lax.all_gather(parts, axes[k], axis=0, tiled=True)
    carried = [lax.axis_size(axes[k]) for k in reversed(turns)]
    parts = parts.reshape(*carried, *shard.shape)
    turned = sorted(range(len(turns)), key=lambda place: turns[len(turns) - 1 - place])
    return parts.transpose(*turned, *range(len(turns), parts.ndim)).reshape(-1, *shard.shape)


def gathered_by_axis(shard, axes, turns, dim):
    return laid_out(all_blocks(shard, axes, turns), dim)


def by_axis(shard, axes):
    return functools.reduce(lax.psum, axes, shard)


def moments(features):
    values = features.astype(jnp.float32)
    return (jnp.sum(values, axis=1), jnp.sum(values * values, axis=1))


def body(
    image_features, text_features, image_gain, text_gain, image_proj, text_proj, pair, logit_scale
):
    row_total = image_features.shape[0]
    shards = lax.axis_size("mp")
    span = row_total // shards
    text_side = lax.axis_index("group") == 1
    first_sum, second_sum = lax.cond(
        text_side, lambda: moments(text_features), lambda: moments(image_features)
    )
    first_sum, second_sum = together((first_sum, second_sum), "mp")
    width = jnp.where(
        text_side, text_features.shape[1] * shards, image_features.shape[1] * shards
    ).astype(jnp.float32)
    average = first_sum / width
    inverse = lax.rsqrt(second_sum / width - average * average + epsilon)

    def apply(features, gain, projection):
        values = features.astype(jnp.float32)
        normed = ((values - average[:, None]) * inverse[:, None] * gain[None, :]).astype(
            jnp.bfloat16
        )
        return jnp.dot(normed, projection, preferred_element_type=jnp.float32)

    embedded = sum_at_owner(
        lax.cond(
            text_side,
            lambda: apply(text_features, text_gain, text_proj),
            lambda: apply(image_features, image_gain, image_proj),
        ),
        "mp",
        0,
    )
    unit = (
        embedded * lax.rsqrt(jnp.sum(embedded * embedded, axis=1, keepdims=True) + 1e-06)
    ).astype(jnp.bfloat16)
    theirs = partner(unit, "group", 0)
    others = lax.all_gather(theirs, DP_MP, axis=0, tiled=True)
    count_all = others.shape[0]
    scores = logit_scale * jnp.einsum("re,ne->rn", unit, others, preferred_element_type=jnp.float32)
    row_peak = jnp.max(scores, axis=1)
    own_total = row_peak + jnp.log(jnp.sum(jnp.exp(scores - row_peak[:, None]), axis=1))
    their_total = partner(own_total, "group", 0)
    other_total = gathered_by_axis(their_total, DP_MP, (1, 0, 3, 2), 0)
    block_index = lax.axis_index(DP) * shards + lax.axis_index("mp")
    row_ids = block_index * span + jnp.arange(span, dtype=jnp.int32)
    column_ids = jnp.arange(count_all, dtype=jnp.int32)
    image_match = jnp.take(pair, row_ids)[:, None] == column_ids[None, :]
    text_match = pair[None, :] == row_ids[:, None]
    flags = jnp.where(text_side, text_match, image_match).astype(jnp.float32)
    target = jnp.sum(flags * scores)
    weights = logit_scale * (
        jnp.exp(scores - own_total[:, None]) + jnp.exp(scores - other_total[None, :]) - 2.0 * flags
    )
    grads = jnp.dot(weights.astype(jnp.bfloat16), others, preferred_element_type=jnp.float32)
    partial_loss = jnp.sum(own_total) - target
    summed = by_axis(partial_loss, GROUP_DP_MP)
    loss = summed / (2.0 * count_all)
    return (grads[None, :, :], loss)


def solution(mesh):
    split = Mesh(
        mesh.devices.reshape(mesh.shape["group"], 4, 4, 2, mesh.shape["mp"]),
        ("group", "dp_0", "dp_1", "dp_2", "mp"),
    )
    placed = (P(DP, "mp"), P(DP, "mp"), P("mp"), P("mp"), P("mp", None), P("mp", None), P(), P())
    return jax.shard_map(
        body, mesh=split, in_specs=placed, out_specs=(P("group", DP_MP, None), P()), check_vma=False
    )
```

profile of v0, /device:TPU:1, one launch (start us, length us, event | category | flops | bytes accessed | tf_op | source)
XLA Modules:
  0.0 265.9 jit_solution(17202370775298530949)
XLA Ops:
  7.2 1.4 conditional.2
  7.2 1.4 fusion
  8.6 0.6 broadcast_in_dim.16
  9.2 4.8 %all-to-all-start = ((f32[4,1,512]{2,1,0:T(1,128)}), f32[4,1,512]{2,1,0:T(1,128)S(1)}, u32[]{:S(2)}, u32[]{:S(2)}) async-start(f32[4,1,512]{2,1,0:T(1,128)} %broadcast_in_dim.16), calls=%async_computation | async-start | bytes 16384 | tf_op jit(solution)/shard_map/all_to_all | solution.py:19
  14.1 4.2 %all-to-all-done = f32[4,1,512]{2,1,0:T(1,128)S(1)} async-done(((f32[4,1,512]{2,1,0:T(1,128)}), f32[4,1,512]{2,1,0:T(1,128)S(1)}, u32[]{:S(2)}, u32[]{:S(2)}) %all-to-all-start) | async-done | bytes 8224 | tf_op jit(solution)/shard_map/all_to_all | solution.py:19
  18.3 3.2 %conditional.3 = (f32[256,1024]{1,0:T(8,128)S(1)}) conditional(s32[]{:T(128)} %convert_element_type.32, (bf16[256,1536]{1,0:T(8,128)(2,1)}, f32[256]{0:T(256)S(1)}, f32[256]{0:T(256)S(1)}, f32[1536]{0:T(1024)}, bf16[1536,1024]{1,0:T(8,128)(2,1)}) %tuple.22, (bf16[256,256]{1,0:T(8,128)(2,1)}, f32[256]{0:T(256)S(1)}, f32[256]{0:T(256)S(1)}, ...), branch_computations={%region_7.8_spmd, %region_8.9_spmd} | conditional | flops 807272448 | bytes 4988936 | solution.py:107
  18.3 3.2 %fusion.2 = f32[256,1024]{1,0:T(8,128)S(1)} fusion(bf16[1536,1024]{1,0:T(8,128)(2,1)} %get-tuple-element.44, bf16[256,1536]{1,0:T(8,128)(2,1)} %get-tuple-element.25, f32[1536]{0:T(1024)} %get-tuple-element.43, f32[256]{0:T(256)S(1)} %get-tuple-element.27, f32[256]{0:T(256)S(1)} %get-tuple-element.26), kind=kOutput, calls=%fused_computation.8 | convolution fusion | flops 807272448 | bytes 4988928 | tf_op jit(solution)/shard_map/cond/branch_0_fun/dot_general | solution.py:104
  21.5 14.6 %all_to_all.11 = f32[4,64,1024]{2,1,0:T(8,128)S(1)} all-to-all(f32[4,64,1024]{2,1,0:T(8,128)S(1)} %bitcast.15), channel_id=1, replica_groups=mesh['group'=2,'dp_0'=4,'dp_1'=4,'dp_2'=2,'mp'=4] {'mp'}, dimensions={0} | all-to-all | bytes 2097152 | tf_op jit(solution)/shard_map/all_to_all | solution.py:45
  36.2 0.1 multiply_reduce_fusion
  36.3 0.1 multiply_convert_fusion.6
  36.4 0.3 collective-permute-start
  36.7 3.6 %collective-permute-done = bf16[64,1024]{1,0:T(8,128)(2,1)S(1)} collective-permute-done((bf16[64,1024]{1,0:T(8,128)(2,1)S(1)}, bf16[64,1024]{1,0:T(8,128)(2,1)S(1)}, u32[]{:S(2)}, u32[]{:S(2)}) %collective-permute-start) | collective-permute-done | bytes 131104 | tf_op jit(solution)/shard_map/ppermute | solution.py:50
  40.3 0.7 copy-done.1
  41.7 0.8 gather_fusion
  42.4 121.1 %all-gather.4.cloned.1.call-done = bf16[8192,1024]{1,0:T(8,128)(2,1)} async-done(((bf16[64,1024]{1,0:T(8,128)(2,1)}), bf16[8192,1024]{1,0:T(8,128)(2,1)}) %all-gather.4.cloned.1.call-update) | async-done | bytes 16777232 | tf_op jit(solution)/shard_map/all_gather | solution.py:119
  163.6 11.0 %fusion.24 = (f32[64]{0:T(128)S(1)}, f32[64,8192]{1,0:T(8,128)S(1)}) fusion(bf16[64,1024]{1,0:T(8,128)(2,1)S(1)} %multiply_convert_fusion.6, bf16[8192,1024]{1,0:T(8,128)(2,1)} %all-gather.4.cloned.1.call-done, f32[]{:T(128)S(6)} %copy.29), kind=kOutput, calls=%fused_computation.50 | convolution fusion | flops 1074790400 | bytes 19005700 | tf_op jit(solution)/shard_map/re,ne->rn/dot_general | solution.py:121
  174.6 1.5 select_reduce_fusion
  176.2 0.6 fusion.23
  176.8 0.7 collective-permute-start.1
  178.8 0.6 dynamic-slice
  179.4 4.3 %psum.35 = f32[]{:T(128)} all-reduce(f32[]{:T(128)S(6)} %sub.60), channel_id=1, replica_groups=mesh['group'=2,'dp_0'=4,'dp_1'=4,'dp_2'=2,'mp'=4] {'group'}, use_global_device_ids=true, to_apply=%region_15.16 | all-reduce | flops 1 | bytes 8 | tf_op jit(solution)/shard_map/psum | solution.py:74
  184.3 9.2 %psum.36 = f32[]{:T(128)} all-reduce(f32[]{:T(128)} %psum.35), channel_id=1, replica_groups=mesh['group'=2,'dp_0'=4,'dp_1'=4,'dp_2'=2,'mp'=4] {'dp_0'}, use_global_device_ids=true, to_apply=%region_16.17 | all-reduce | flops 1 | bytes 8 | tf_op jit(solution)/shard_map/psum | solution.py:74
  193.5 0.2 dynamic-update-slice
  193.7 9.9 %all-reduce.1 = (f32[256]{0:T(256)S(1)}, f32[]{:T(128)}) all-reduce(f32[256]{0:T(256)S(1)} %dynamic-update-slice, f32[]{:T(128)} %psum.36), channel_id=2, replica_groups=mesh['group'=2,'dp_0'=4,'dp_1'=4,'dp_2'=2,'mp'=4] {'dp_1'}, use_global_device_ids=true, to_apply=%add | all-reduce | flops 257 | bytes 2056
  203.6 8.5 %psum.38 = f32[]{:T(128)} all-reduce(f32[]{:T(128)} %get-tuple-element.56), channel_id=1, replica_groups=mesh['group'=2,'dp_0'=4,'dp_1'=4,'dp_2'=2,'mp'=4] {'dp_2'}, use_global_device_ids=true, to_apply=%region_18.19 | all-reduce | flops 1 | bytes 8 | tf_op jit(solution)/shard_map/psum | solution.py:74
  212.1 8.9 %psum.39 = f32[]{:T(128)} all-reduce(f32[]{:T(128)} %psum.38), channel_id=1, replica_groups=mesh['group'=2,'dp_0'=4,'dp_1'=4,'dp_2'=2,'mp'=4] {'mp'}, use_global_device_ids=true, to_apply=%region_19.20 | all-reduce | flops 1 | bytes 8 | tf_op jit(solution)/shard_map/psum | solution.py:74
  221.0 0.1 reshape.82
  221.1 8.1 %all-gather.1 = f32[4,4,64]{2,1,0:T(4,128)S(1)} all-gather(f32[1,4,64]{2,1,0:T(4,128)S(1)} %reshape.82), channel_id=1, replica_groups=mesh['group'=2,'dp_0'=4,'dp_1'=4,'dp_2'=2,'mp'=4] {'dp_0'}, dimensions={0}, use_global_device_ids=true | all-gather | bytes 5120 | tf_op jit(solution)/shard_map/all_gather | solution.py:62
  229.2 9.0 %all_gather.18 = f32[64,64]{1,0:T(8,128)S(1)} all-gather(f32[16,64]{1,0:T(8,128)S(1)} %bitcast.17), channel_id=1, replica_groups=mesh['group'=2,'dp_0'=4,'dp_1'=4,'dp_2'=2,'mp'=4] {'mp'}, dimensions={0}, use_global_device_ids=true | all-gather | bytes 20480 | tf_op jit(solution)/shard_map/all_gather | solution.py:62
  238.2 9.0 %all_gather.19 = f32[128,64]{1,0:T(8,128)S(1)} all-gather(f32[64,64]{1,0:T(8,128)S(1)} %all_gather.18), channel_id=1, replica_groups=mesh['group'=2,'dp_0'=4,'dp_1'=4,'dp_2'=2,'mp'=4] {'dp_2'}, dimensions={0}, use_global_device_ids=true | all-gather | bytes 49152 | tf_op jit(solution)/shard_map/all_gather | solution.py:62
  247.3 0.1 sub.56
  248.0 9.9 %convolution_bitcast_fusion = f32[1,64,1024]{2,1,0:T(8,128)} fusion(bf16[8192,1024]{1,0:T(8,128)(2,1)} %all-gather.4.cloned.1.call-done, f32[64,8192]{1,0:T(8,128)S(1)} %get-tuple-element.62, s32[64]{0:T(128)S(1)} %get-tuple-element.63, s32[8192]{0:T(1024)S(1)} %copy-done, f32[8192]{0:T(1024)S(1)} %sub.56, f32[64]{0:T(128)S(1)} %get-tuple-element.58, ...), kind=kOutput, calls=%fused_computation.23 | convolution fusion | flops 1078984704 | bytes 19202820 | tf_op jit(solution)/shard_map/dot_general | solution.py:136
  (18 shorter events, 0.2 us)
Async XLA Ops:
  9.2 9.0 %all-to-all-start = ((f32[4,1,512]{2,1,0:T(1,128)}), f32[4,1,512]{2,1,0:T(1,128)S(1)}, u32[]{:S(2)}, u32[]{:S(2)}) async-start(f32[4,1,512]{2,1,0:T(1,128)} %broadcast_in_dim.16), calls=%async_computation | async-start | bytes 16384 | tf_op jit(solution)/shard_map/all_to_all | solution.py:19
  14.1 149.5 %all-gather.4.cloned.1.call-start = ((), (), s32[]{:S(2)}) async-start(), calls=%async_computation.2 | async-start | bytes 16908288 | tf_op jit(solution)/shard_map/all_gather | solution.py:119
  21.5 20.2 %copy-start = (s32[8192]{0:T(1024)S(1)}, s32[8192]{0:T(1024)}, u32[]{:S(2)}) copy-start(s32[8192]{0:T(1024)} %param.18) | copy-start | bytes 98308
  36.4 3.9 %collective-permute-start = (bf16[64,1024]{1,0:T(8,128)(2,1)S(1)}, bf16[64,1024]{1,0:T(8,128)(2,1)S(1)}, u32[]{:S(2)}, u32[]{:S(2)}) collective-permute-start(bf16[64,1024]{1,0:T(8,128)(2,1)S(1)} %multiply_convert_fusion.6), channel_id=1, source_target_pairs={{0,128},{128,0},{1,129},{129,1},{2,130},{130,2},{3,131},{131,3},{4... | collective-permute-start | bytes 393224 | tf_op jit(solution)/shard_map/ppermute | solution.py:50
  40.3 0.7 copy-start.1
  174.6 4.2 %copy-start.2 = (u32[256]{0:T(256)S(1)}, u32[256]{0:T(256)}, u32[]{:S(2)}) copy-start(u32[256]{0:T(256)} %constant.71) | copy-start | bytes 3076
  176.8 16.7 %collective-permute-start.1 = (f32[64]{0:T(128)S(1)}, f32[64]{0:T(128)S(1)}, u32[]{:S(2)}, u32[]{:S(2)}) collective-permute-start(f32[64]{0:T(128)S(1)} %get-tuple-element.58), channel_id=1, source_target_pairs={{0,128},{128,0},{1,129},{129,1},{2,130},{130,2},{3,131},{131,3},{4... | collective-permute-start | bytes 776 | tf_op jit(solution)/shard_map/ppermute | solution.py:50
Sparse Core Ops, SparseCore 0:
  41.1 122.4 all-gather.3
where the time goes:
time: 266 us
  waiting for transfers between devices  129 us (48%)
  blocking collectives  81.5 us (31%)
  matrix products  24.1 us (9%)
  between operations  18.5 us (7%)
  starting transfers between devices  5.82 us (2%)
  other arithmetic  3.92 us (1%)
  local copies, waits for them, and re-layouts  3.02 us (1%)
    all_gather x1, waiting for transfers between devices, body(): others = lax.all_gather(theirs, DP_MP, axis=0, tiled=True)  121 us
    psum x4, blocking collectives, by_axis(): return functools.reduce(lax.psum, axes, shard)  30.8 us
    all_gather x3, blocking collectives, all_blocks(): parts = lax.all_gather(parts, axes[k], axis=0, tiled=True)  26.2 us
    all_to_all x1, blocking collectives, sum_at_owner(): parts = lax.all_to_all(in_blocks(shard, dim, peers), axis, 0, 0, tiled=True)  14.6 us
    dot_general x1, matrix products, body(): jnp.einsum('re,ne->rn', unit, others, preferred_element_type=jnp.float32)  11 us
    unnamed x1, blocking collectives  9.94 us
    dot_general x1, matrix products, body(): jnp.dot(weights.astype(jnp.bfloat16), others, preferred_element_type=jnp....  9.9 us
  transfers between devices with their start and end apart: 4, of which 3 were waited for; matrix products, arithmetic and copies ran while one was open for 1% of the time, Pallas kernels for 0%

commit v1 on v0

v1 whole, which is shorter than its diff:
```python
import functools

import jax
import jax.numpy as jnp
from jax import lax
from jax.experimental import pallas as pl
from jax.experimental.pallas import tpu as pltpu
from jax.sharding import Mesh
from jax.sharding import PartitionSpec as P

DP_MP = ("dp_0", "dp_1", "dp_2", "mp")
DP = ("dp_0", "dp_1", "dp_2")
MESH = pl.DeviceIdType.MESH

X, Y, ZH, ZL, C = 4, 4, 4, 2, 2
Z = ZH * ZL
XY = X * Y
ZC = Z * C
PIECE = 32
HALF = X * PIECE
BLOCK = XY * PIECE
ROWS = 2 * PIECE
SIDE = Z * PIECE

epsilon = 1e-05
f32 = jnp.float32
bf16 = jnp.bfloat16


def dot(a, b, dims=((1,), (0,))):
    return lax.dot_general(a, b, (dims, ((), ())), preferred_element_type=f32)


def each(low, high, step):
    def turn(i, carry):
        step(i)
        return carry

    lax.fori_loop(low, high, turn, 0)


def kernel(
    feat_i, feat_t, gain_i, gain_t, proj_i, proj_t, pair, scale_ref,
    out, loss_out,
    fi, ft, pi, pt, stats, part_i, part_t, own_i, own_t, got_i, got_t,
    ibuf, tbuf, scores, weights, lse_r, lse_c, loss_1, loss_2,
    img_d2d, img_d2d_got, img_send, img_own, img_got, txt_send, txt_got, fin, fin_got,
    load_sem, stat_s, stat_r, rsi_s, rsi_r, rst_s, rst_r,
    agi_s, agi_r, fwd_s, fwd_r, agt_s, agt_r,
    lr_s, lr_r, lc_s, lc_r, l1_s, l1_r, l2_s, l2_r,
    d2d_s, d2d_r, gi_s, gi_r, gt_s, gt_r, fin_s, fin_r,
):
    x, y = lax.axis_index("mp"), lax.axis_index("dp_0")
    zh, c, zl = lax.axis_index("dp_1"), lax.axis_index("dp_2"), lax.axis_index("group")
    z = zh * ZL + zl
    xy = y * X + x
    zc = c * Z + z

    def remote(src, dst, send, recv, **where):
        return pltpu.make_async_remote_copy(
            src_ref=src, dst_ref=dst, send_sem=send, recv_sem=recv,
            device_id=where, device_id_type=MESH,
        )

    def plane(d):
        return {"mp": (x + d % X) % X, "dp_0": (y + d // X) % Y}

    def column(d):
        there = (z + d % Z) % Z
        return {"dp_1": there // ZL, "group": there % ZL, "dp_2": (c + d // Z) % C}

    loads = []
    for k in range(X):
        rows = pl.ds(pl.multiple_of(k * ROWS + zl * PIECE, PIECE), PIECE)
        here = pl.ds(k * PIECE, PIECE)
        loads.append(pltpu.make_async_copy(feat_i.at[rows], fi.at[here], load_sem.at[k]))
        loads.append(pltpu.make_async_copy(feat_t.at[rows], ft.at[here], load_sem.at[X + k]))
    loads_p = [
        pltpu.make_async_copy(proj_t, pt, load_sem.at[2 * X]),
        pltpu.make_async_copy(proj_i, pi, load_sem.at[2 * X + 1]),
    ]
    for copy in loads + loads_p:
        copy.start()

    barrier = pltpu.get_barrier_semaphore()

    def greet_plane(d):
        pl.semaphore_signal(barrier, inc=1, device_id=plane(d), device_id_type=MESH)

    def greet_column(d):
        pl.semaphore_signal(barrier, inc=1, device_id=column(d), device_id_type=MESH)

    each(1, XY, greet_plane)
    each(1, ZC, greet_column)

    for copy in loads:
        copy.wait()
    vi = fi[...].astype(f32)
    vt = ft[...].astype(f32)
    lane = lax.broadcasted_iota(jnp.int32, (HALF, 128), 1)
    packed = jnp.where(lane == 0, jnp.sum(vi, axis=1, keepdims=True), 0.0)
    packed = jnp.where(lane == 1, jnp.sum(vi * vi, axis=1, keepdims=True), packed)
    packed = jnp.where(lane == 2, jnp.sum(vt, axis=1, keepdims=True), packed)
    packed = jnp.where(lane == 3, jnp.sum(vt * vt, axis=1, keepdims=True), packed)
    stats[x] = packed.T[:8]

    pl.semaphore_wait(barrier, XY - 1 + ZC - 1)

    def stat_copy(d):
        return remote(stats.at[x], stats.at[x], stat_s.at[d], stat_r.at[d], mp=(x + d) % X)

    each(1, X, lambda d: stat_copy(d).start())
    each(1, X, lambda d: stat_copy(d).wait_recv())
    total = stats[0] + stats[1] + stats[2] + stats[3]
    total = jnp.concatenate([total] * 16, axis=0).T

    def normed(values, first, width, gain):
        average = total[:, first : first + 1] / width
        inverse = lax.rsqrt(total[:, first + 1 : first + 2] / width - average * average + epsilon)
        return ((values - average) * inverse * gain).astype(bf16)

    def share_copy(d, part, got, send, recv):
        there = (x + d) % X
        rows = pl.ds(pl.multiple_of(there * PIECE, PIECE), PIECE)
        return remote(part.at[rows], got.at[d], send.at[d], recv.at[d], mp=there)

    share_t = lambda d: share_copy(d, part_t, got_t, rst_s, rst_r)
    share_i = lambda d: share_copy(d, part_i, got_i, rsi_s, rsi_r)
    loads_p[0].wait()
    value = dot(normed(ft[...].astype(f32), 2, f32(X * ft.shape[1]), gain_t[...]), pt[...])
    own_t[...] = value
    part_t[...] = value.astype(bf16)
    each(1, X, lambda d: share_t(d).start())
    loads_p[1].wait()
    value = dot(normed(fi[...].astype(f32), 0, f32(X * fi.shape[1]), gain_i[...]), pi[...])
    own_i[...] = value
    part_i[...] = value.astype(bf16)
    each(1, X, lambda d: share_i(d).start())

    def unit_of(own, got):
        value = own[pl.ds(pl.multiple_of(x * PIECE, PIECE), PIECE)]
        for d in range(1, X):
            value = value + got[d].astype(f32)
        return (value * lax.rsqrt(jnp.sum(value * value, axis=1, keepdims=True) + 1e-06)).astype(bf16)

    def slot(buffer, index):
        return buffer.at[pl.ds(pl.multiple_of(index * PIECE, PIECE), PIECE)]

    def text_copy(d):
        mine = slot(tbuf, xy)
        return remote(mine, mine, agt_s.at[d], agt_r.at[d], **plane(d))

    def image_copy(d):
        mine = slot(ibuf, zc)
        return remote(mine, mine, agi_s.at[d], agi_r.at[d], **column(d))

    def forward(d):
        held = slot(ibuf, c * Z + (z + Z - d) % Z)
        return remote(held, held, fwd_s.at[d], fwd_r.at[d], dp_2=1 - c)

    each(1, X, lambda d: share_t(d).wait_recv())
    tbuf[pl.ds(pl.multiple_of(xy * PIECE, PIECE), PIECE)] = unit_of(own_t, got_t)
    each(1, XY, lambda d: text_copy(d).start())
    each(1, X, lambda d: share_i(d).wait_recv())
    ibuf[pl.ds(pl.multiple_of(zc * PIECE, PIECE), PIECE)] = unit_of(own_i, got_i)
    each(1, Z, lambda d: image_copy(d).start())
    forward(0).start()
    for d in (1, 7, 2, 6, 3, 5, 4):
        image_copy(d).wait_recv()
        forward(d).start()
    each(0, Z, lambda d: forward(d).wait_recv())
    each(1, XY, lambda d: text_copy(d).wait_recv())

    scale = scale_ref[0, 0]
    quarters = [pl.ds(k * 128, 128) for k in range(BLOCK // 128)]
    packed = jnp.zeros((128, 128), f32)
    peak_c = None
    for k, rows in enumerate(quarters):
        s = scale * dot(ibuf[rows], tbuf[...], ((1,), (1,)))
        scores[rows] = s
        peak = jnp.max(s, axis=1, keepdims=True)
        log_sum = peak + jnp.log(jnp.sum(jnp.exp(s - peak), axis=1, keepdims=True))
        packed = jnp.where(lane == k, log_sum, packed)
        high = jnp.max(s, axis=0, keepdims=True)
        peak_c = high if peak_c is None else jnp.maximum(peak_c, high)
    lse_r[zc] = packed.T[:8]

    def lse_r_copy(d):
        return remote(lse_r.at[zc], lse_r.at[zc], lr_s.at[d], lr_r.at[d], **column(d))

    def lse_c_copy(d):
        return remote(lse_c.at[xy], lse_c.at[xy], lc_s.at[d], lc_r.at[d], **plane(d))

    each(1, ZC, lambda d: lse_r_copy(d).start())
    sum_c = jnp.zeros((1, BLOCK), f32)
    for rows in quarters:
        sum_c = sum_c + jnp.sum(jnp.exp(scores[rows] - peak_c), axis=0, keepdims=True)
    log_sum = peak_c + jnp.log(sum_c)

    def as_tile(line):
        return jnp.concatenate(
            [line[:, k * 128 : (k + 1) * 128] for k in range(4)] + [jnp.zeros((4, 128), f32)], axis=0
        )

    lse_c[xy] = as_tile(log_sum)
    each(1, XY, lambda d: lse_c_copy(d).start())

    def combined(parts):
        values = parts[...]
        peak = jnp.max(values, axis=0)
        return peak + jnp.log(jnp.sum(jnp.exp(values - peak[None]), axis=0))

    held = pair[pl.ds(y * 16 + x // 2, 8, stride=2), :]
    held = jnp.where(x % 2 == 1, pltpu.roll(held, 64, 1), held)
    held = jnp.concatenate([held] * 16, axis=0).T
    captions = jnp.concatenate([held[:64, h * C + k : h * C + k + 1] for k in range(C) for h in range(ZH)], axis=0)
    j = lax.broadcasted_iota(jnp.int32, (1, BLOCK), 1)
    ids = ((j // 128) * 8 + zh * C + c) * 256 + ((j // PIECE) % X) * ROWS + zl * PIECE + j % PIECE

    each(1, ZC, lambda d: lse_r_copy(d).wait_recv())
    total_r = combined(lse_r)
    turned = jnp.concatenate([total_r] * 16, axis=0).T
    each(1, XY, lambda d: lse_c_copy(d).wait_recv())
    total_c = combined(lse_c)
    line_c = jnp.concatenate([total_c[k : k + 1] for k in range(4)], axis=1)
    target = jnp.zeros((1, BLOCK), f32)
    for k, rows in enumerate(quarters):
        s = scores[rows]
        flags = (captions[k * 128 : (k + 1) * 128] == ids).astype(f32)
        target = target + jnp.sum(flags * s, axis=0, keepdims=True)
        w = scale * (jnp.exp(s - turned[:, k : k + 1]) + jnp.exp(s - line_c) - 2.0 * flags)
        weights[rows] = w.astype(bf16)
    row = lax.broadcasted_iota(jnp.int32, (8, 128), 0)
    shared = jnp.where(row < 4, total_r + total_c, 0.0) * (1.0 / 16)
    loss_1[zc] = shared - 2.0 * as_tile(target)

    def loss_1_copy(d):
        return remote(loss_1.at[zc], loss_1.at[zc], l1_s.at[d], l1_r.at[d], **column(d))

    def loss_2_copy(d):
        return remote(loss_2.at[xy], loss_2.at[xy], l2_s.at[d], l2_r.at[d], **plane(d))

    each(1, ZC, lambda d: loss_1_copy(d).start())

    d2d = remote(img_d2d, img_d2d_got, d2d_s, d2d_r, dp_2=1 - c)
    rows = pl.ds(pl.multiple_of((1 - c) * SIDE, SIDE), SIDE)
    img_d2d[...] = dot(weights[rows], tbuf[...]).astype(bf16)
    d2d.start()

    def grad_t_copy(d):
        there = plane(d)
        piece = slot(txt_send, there["dp_0"] * X + there["mp"])
        return remote(piece, txt_got.at[d], gt_s.at[d], gt_r.at[d], **there)

    for k in range(4):
        cols = pl.ds(k * 128, 128)
        txt_send[cols] = dot(weights[:, cols], ibuf[...], ((0,), (0,))).astype(bf16)
    each(1, XY, lambda d: grad_t_copy(d).start())

    def grad_i_copy(d):
        there = (zh + d) % ZH
        piece = img_send.at[pl.ds(pl.multiple_of(there * ROWS, ROWS), ROWS)]
        gap = (there * ZL + Z - z) % Z
        return remote(piece, img_got.at[gap], gi_s.at[d], gi_r.at[gap], dp_1=there, group=0)

    rows = pl.ds(pl.multiple_of(c * SIDE, SIDE), SIDE)
    value = dot(weights[rows], tbuf[...])
    d2d.wait_recv()
    value = value + img_d2d_got[...].astype(f32)
    img_own[...] = value
    img_send[...] = value.astype(bf16)

    @pl.when(zl == 1)
    def _():
        grad_i_copy(0).start()

    each(1, ZH, lambda d: grad_i_copy(d).start())

    each(1, ZC, lambda d: loss_1_copy(d).wait_recv())
    loss_2[xy] = jnp.sum(loss_1[...], axis=0)
    each(1, XY, lambda d: loss_2_copy(d).start())

    each(1, XY, lambda d: grad_t_copy(d).wait_recv())
    value = txt_send[pl.ds(pl.multiple_of(xy * PIECE, PIECE), PIECE)].astype(f32)
    for d in range(1, XY):
        value = value + txt_got[d].astype(f32)

    last = remote(fin, fin_got, fin_s, fin_r, group=1)

    @pl.when(zl == 0)
    def _():
        fin[...] = value.astype(bf16)
        last.start()
        own = img_own[pl.ds(pl.multiple_of(zh * ROWS, ROWS), ROWS)]

        def arrived(gap):
            remote(img_send.at[:ROWS], img_got.at[gap], gi_s.at[0], gi_r.at[gap], group=0).wait_recv()

        each(1, Z, arrived)
        for gap in range(1, Z):
            own = own + img_got[gap].astype(f32)
        out[0] = own
        last.wait_send()

    @pl.when(zl == 1)
    def _():
        out[0, PIECE:] = value
        grad_i_copy(0).wait_send()
        last.wait_recv()
        out[0, :PIECE] = fin_got[...].astype(f32)

    each(1, XY, lambda d: loss_2_copy(d).wait_recv())
    loss_out[0, 0] = jnp.sum(jnp.sum(loss_2[...], axis=0)) * (1.0 / (2 * XY * BLOCK))

    def sent_x(d):
        stat_copy(d).wait_send()
        share_t(d).wait_send()
        share_i(d).wait_send()
        grad_i_copy(d).wait_send()

    def sent_plane(d):
        text_copy(d).wait_send()
        lse_r_copy(d).wait_send()
        lse_c_copy(d).wait_send()
        loss_1_copy(d).wait_send()
        loss_2_copy(d).wait_send()
        grad_t_copy(d).wait_send()

    each(1, X, sent_x)
    each(1, Z, lambda d: image_copy(d).wait_send())
    each(0, Z, lambda d: forward(d).wait_send())
    each(1, XY, sent_plane)
    d2d.wait_send()


def body(
    image_features, text_features, image_gain, text_gain, image_proj, text_proj, pair, logit_scale
):
    width_i, width_t = image_features.shape[1], text_features.shape[1]
    emb = image_proj.shape[1]
    vmem = pl.BlockSpec(memory_space=pltpu.VMEM)
    smem = pl.BlockSpec(memory_space=pltpu.SMEM)
    hbm = pl.BlockSpec(memory_space=pl.ANY)
    dma = lambda *n: pltpu.SemaphoreType.DMA(n)
    grads, loss = pl.pallas_call(
        kernel,
        out_shape=(
            jax.ShapeDtypeStruct((1, ROWS, emb), f32),
            jax.ShapeDtypeStruct((1, 1), f32),
        ),
        in_specs=[hbm, hbm, vmem, vmem, hbm, hbm, vmem, smem],
        out_specs=(vmem, smem),
        scratch_shapes=[
            pltpu.VMEM((HALF, width_i), bf16),
            pltpu.VMEM((HALF, width_t), bf16),
            pltpu.VMEM((width_i, emb), bf16),
            pltpu.VMEM((width_t, emb), bf16),
            pltpu.VMEM((X, 8, 128), f32),
            pltpu.VMEM((HALF, emb), bf16),
            pltpu.VMEM((HALF, emb), bf16),
            pltpu.VMEM((HALF, emb), f32),
            pltpu.VMEM((HALF, emb), f32),
            pltpu.VMEM((X, PIECE, emb), bf16),
            pltpu.VMEM((X, PIECE, emb), bf16),
            pltpu.VMEM((BLOCK, emb), bf16),
            pltpu.VMEM((BLOCK, emb), bf16),
            pltpu.VMEM((BLOCK, BLOCK), f32),
            pltpu.VMEM((BLOCK, BLOCK), bf16),
            pltpu.VMEM((ZC, 8, 128), f32),
            pltpu.VMEM((XY, 8, 128), f32),
            pltpu.VMEM((ZC, 8, 128), f32),
            pltpu.VMEM((XY, 8, 128), f32),
            pltpu.VMEM((SIDE, emb), bf16),
            pltpu.VMEM((SIDE, emb), bf16),
            pltpu.VMEM((SIDE, emb), bf16),
            pltpu.VMEM((SIDE, emb), f32),
            pltpu.VMEM((Z, ROWS, emb), bf16),
            pltpu.VMEM((BLOCK, emb), bf16),
            pltpu.VMEM((XY, PIECE, emb), bf16),
            pltpu.VMEM((PIECE, emb), bf16),
            pltpu.VMEM((PIECE, emb), bf16),
            dma(2 * X + 2),
            dma(X), dma(X), dma(X), dma(X), dma(X), dma(X),
            dma(Z), dma(Z), dma(Z), dma(Z), dma(XY), dma(XY),
            dma(ZC), dma(ZC), dma(XY), dma(XY), dma(ZC), dma(ZC), dma(XY), dma(XY),
            pltpu.SemaphoreType.DMA, pltpu.SemaphoreType.DMA,
            dma(ZH), dma(Z), dma(XY), dma(XY),
            pltpu.SemaphoreType.DMA, pltpu.SemaphoreType.DMA,
        ],
        compiler_params=pltpu.CompilerParams(
            collective_id=0, has_side_effects=True, vmem_limit_bytes=48 * 1024 * 1024
        ),
        name="contrastive",
    )(
        image_features, text_features, image_gain.reshape(1, -1), text_gain.reshape(1, -1),
        image_proj, text_proj, pair.reshape(-1, 128), logit_scale.reshape(1, 1),
    )
    return grads, loss.reshape(())


def solution(mesh):
    split = Mesh(
        mesh.devices.reshape(mesh.shape["group"], 4, 4, 2, mesh.shape["mp"]),
        ("group", "dp_0", "dp_1", "dp_2", "mp"),
    )
    placed = (P(DP, "mp"), P(DP, "mp"), P("mp"), P("mp"), P("mp", None), P("mp", None), P(), P())
    return jax.shard_map(
        body, mesh=split, in_specs=placed, out_specs=(P("group", DP_MP, None), P()), check_vma=False
    )
```

time: 266 us -> 82.4 us (0.31)
  waiting for transfers between devices: 129 us -> 0 us
  blocking collectives: 81.5 us -> 0 us
  Pallas kernels: 0 us -> 70.6 us
  matrix products: 24.1 us -> 0 us
  between operations: 18.5 us -> 3.11 us
  starting transfers between devices: 5.82 us -> 0 us
  local copies, waits for them, and re-layouts: 3.02 us -> 7.81 us
  other arithmetic: 3.92 us -> 0 us
    all_gather x1 -> x0, waiting for transfers between devices: 121 us -> none  [body(): others = lax.all_gather(theirs, DP_MP, axis=0, tiled=True)]
    pallas_call x0 -> x1, Pallas kernels: none -> 70.6 us  [body(): pl.pallas_call(kernel, out_shape=(jax.ShapeDtypeStruct((1, ROWS, emb), f3...]
    psum x4 -> x0, blocking collectives: 30.8 us -> none  [by_axis(): return functools.reduce(lax.psum, axes, shard)]
    all_gather x3 -> x0, blocking collectives: 26.2 us -> none  [all_blocks(): parts = lax.all_gather(parts, axes[k], axis=0, tiled=True)]
    dot_general x3 -> x0, matrix products: 24.1 us -> none  [the longest x1 11 us: body(): jnp.einsum('re,ne->rn', unit, others, preferred_element_type=jnp.float32)]
    all_to_all x1 -> x0, blocking collectives: 14.6 us -> none  [sum_at_owner(): parts = lax.all_to_all(in_blocks(shard, dim, peers), axis, 0, 0, tiled=True)]
    unnamed x1 -> x0, blocking collectives: 9.94 us -> none
    unnamed x10 -> x13, local copies, waits for them, and re-layouts: 1.53 us -> 7.11 us
  transfers between devices with their start and end apart: 4 -> 0, of which waited for: 3 -> 0; matrix products, arithmetic and copies ran while one was open for 1% -> 0% of each run, Pallas kernels for 0% -> 0%
where the time goes in v1:
time: 82.4 us; the launch traced here: 81.5 us
  Pallas kernels  70.6 us (86%)
  local copies, waits for them, and re-layouts  7.81 us (9%)
  between operations  3.11 us (4%)
    pallas_call x1, Pallas kernels, body(): pl.pallas_call(kernel, out_shape=(jax.ShapeDtypeStruct((1, ROWS, emb), f3...  70.6 us
    unnamed x13, local copies, waits for them, and re-layouts  7.11 us

profile of v1, /device:TPU:1, one launch (start us, length us, event | category | flops | bytes accessed | tf_op | source)
XLA Modules:
  0.0 81.5 jit_solution(4180960873488564583)
XLA Ops:
  1.3 0.7 reshape.19.gain_i
  2.0 0.0 copy-start
  2.0 1.9 %copy-done = bf16[1536,1024]{1,0:T(8,128)(2,1)S(1)} copy-done((bf16[1536,1024]{1,0:T(8,128)(2,1)S(1)}, bf16[1536,1024]{1,0:T(8,128)(2,1)}, u32[]{:S(2)}) %copy-start) | copy-done | bytes 3145752
  3.9 0.0 copy-start.1
  3.9 1.1 %copy-done.1 = bf16[256,1536]{1,0:T(8,128)(2,1)S(1)} copy-done((bf16[256,1536]{1,0:T(8,128)(2,1)S(1)}, bf16[256,1536]{1,0:T(8,128)(2,1)}, u32[]{:S(2)}) %copy-start.1) | copy-done | bytes 786456
  5.0 0.0 copy-start.2
  5.0 1.0 %copy-done.2 = bf16[256,1024]{1,0:T(8,128)(2,1)S(1)} copy-done((bf16[256,1024]{1,0:T(8,128)(2,1)S(1)}, bf16[256,1024]{1,0:T(8,128)(2,1)}, u32[]{:S(2)}) %copy-start.2) | copy-done | bytes 524312
  6.0 0.0 copy-start.3
  6.0 0.9 %copy-done.3 = bf16[256,256]{1,0:T(8,128)(2,1)S(1)} copy-done((bf16[256,256]{1,0:T(8,128)(2,1)S(1)}, bf16[256,256]{1,0:T(8,128)(2,1)}, u32[]{:S(2)}) %copy-start.3) | copy-done | bytes 131096
  6.9 0.0 copy-start.4
  7.0 0.8 copy-done.4
  7.7 0.0 copy-start.5
  7.7 0.7 copy-done.5
  8.4 70.6 %contrastive.1 = (f32[1,64,1024]{2,1,0:T(8,128)S(1)}, f32[1,1]{1,0:T(1,128)}) custom-call(bf16[256,1536]{1,0:T(8,128)(2,1)S(1)} %copy-done.1, bf16[256,256]{1,0:T(8,128)(2,1)S(1)} %copy-done.3, f32[1,1536]{1,0:T(1,128)S(1)} %reshape.19.gain_i, f32[1,256]{1,0:T(1,128)S(1)} %bitcast.6, bf16[1536,1024]{1,0:T(8,128)(2,1)S(1)} %copy-done, ...), custom_call_target="tpu_custom_call" | custom-call | tf_op jit(solution)/shard_map/contrastive/pallas_call | solution.py:345
  79.0 0.7 copy.13
Async XLA Ops:
  2.0 1.9 %copy-start = (bf16[1536,1024]{1,0:T(8,128)(2,1)S(1)}, bf16[1536,1024]{1,0:T(8,128)(2,1)}, u32[]{:S(2)}) copy-start(bf16[1536,1024]{1,0:T(8,128)(2,1)} %proj_i.1) | copy-start | bytes 9437188
  3.9 1.1 %copy-start.1 = (bf16[256,1536]{1,0:T(8,128)(2,1)S(1)}, bf16[256,1536]{1,0:T(8,128)(2,1)}, u32[]{:S(2)}) copy-start(bf16[256,1536]{1,0:T(8,128)(2,1)} %feat_i.1) | copy-start | bytes 2359300
  5.0 1.0 %copy-start.2 = (bf16[256,1024]{1,0:T(8,128)(2,1)S(1)}, bf16[256,1024]{1,0:T(8,128)(2,1)}, u32[]{:S(2)}) copy-start(bf16[256,1024]{1,0:T(8,128)(2,1)} %proj_t.1) | copy-start | bytes 1572868
  6.0 0.9 %copy-start.3 = (bf16[256,256]{1,0:T(8,128)(2,1)S(1)}, bf16[256,256]{1,0:T(8,128)(2,1)}, u32[]{:S(2)}) copy-start(bf16[256,256]{1,0:T(8,128)(2,1)} %feat_t.1) | copy-start | bytes 393220
  6.9 0.8 copy-start.4
  7.7 0.7 copy-start.5

commit v2 on v1

--- a/solution.py
+++ b/solution.py
@@ -40,9 +40,9 @@
 
 
 def kernel(
-    feat_i, feat_t, gain_i, gain_t, proj_i, proj_t, pair, scale_ref,
+    feat_i, feat_t, gain_i, gain_t, proj_i, proj_t, pair_hbm, scale_ref,
     out, loss_out,
-    fi, ft, pi, pt, stats, part_i, part_t, own_i, own_t, got_i, got_t,
+    fi, ft, gi, gt, pair, pi, pt, lhs_i, lhs_t, stats, moments, part_i, part_t, own_i, own_t, got_i, got_t,
     ibuf, tbuf, scores, weights, lse_r, lse_c, loss_1, loss_2,
     img_d2d, img_d2d_got, img_send, img_own, img_got, txt_send, txt_got, fin, fin_got,
     load_sem, stat_s, stat_r, rsi_s, rsi_r, rst_s, rst_r,
@@ -75,11 +75,16 @@
         here = pl.ds(k * PIECE, PIECE)
         loads.append(pltpu.make_async_copy(feat_i.at[rows], fi.at[here], load_sem.at[k]))
         loads.append(pltpu.make_async_copy(feat_t.at[rows], ft.at[here], load_sem.at[X + k]))
+    loads += [
+        pltpu.make_async_copy(gain_i, gi, load_sem.at[2 * X + 2]),
+        pltpu.make_async_copy(gain_t, gt, load_sem.at[2 * X + 3]),
+    ]
     loads_p = [
         pltpu.make_async_copy(proj_t, pt, load_sem.at[2 * X]),
         pltpu.make_async_copy(proj_i, pi, load_sem.at[2 * X + 1]),
     ]
-    for copy in loads + loads_p:
+    load_pair = pltpu.make_async_copy(pair_hbm, pair, load_sem.at[2 * X + 4])
+    for copy in loads + loads_p + [load_pair]:
         copy.start()
 
     barrier = pltpu.get_barrier_semaphore()
@@ -95,29 +100,22 @@
 
     for copy in loads:
         copy.wait()
-    vi = fi[...].astype(f32)
-    vt = ft[...].astype(f32)
     lane = lax.broadcasted_iota(jnp.int32, (HALF, 128), 1)
-    packed = jnp.where(lane == 0, jnp.sum(vi, axis=1, keepdims=True), 0.0)
-    packed = jnp.where(lane == 1, jnp.sum(vi * vi, axis=1, keepdims=True), packed)
-    packed = jnp.where(lane == 2, jnp.sum(vt, axis=1, keepdims=True), packed)
-    packed = jnp.where(lane == 3, jnp.sum(vt * vt, axis=1, keepdims=True), packed)
-    stats[x] = packed.T[:8]
-
-    pl.semaphore_wait(barrier, XY - 1 + ZC - 1)
-
-    def stat_copy(d):
-        return remote(stats.at[x], stats.at[x], stat_s.at[d], stat_r.at[d], mp=(x + d) % X)
-
-    each(1, X, lambda d: stat_copy(d).start())
-    each(1, X, lambda d: stat_copy(d).wait_recv())
-    total = stats[0] + stats[1] + stats[2] + stats[3]
-    total = jnp.concatenate([total] * 16, axis=0).T
-
-    def normed(values, first, width, gain):
-        average = total[:, first : first + 1] / width
-        inverse = lax.rsqrt(total[:, first + 1 : first + 2] / width - average * average + epsilon)
-        return ((values - average) * inverse * gain).astype(bf16)
+    row = lax.broadcasted_iota(jnp.int32, (8, 128), 0)
+
+    def centred(features, gain, lhs):
+        values = features[...].astype(f32)
+        mean = jnp.sum(values, axis=1, keepdims=True) * (1.0 / values.shape[1])
+        squares = jnp.sum(values * values, axis=1, keepdims=True)
+        line = jnp.concatenate([gain[k : k + 1, :] for k in range(gain.shape[0])], axis=1)
+        lhs[:HALF] = ((values - mean) * line).astype(bf16)
+        coarse = line.astype(bf16)
+        fine = (line - coarse.astype(f32)).astype(bf16)
+        lhs[HALF:] = jnp.concatenate([coarse, fine, jnp.zeros((14, line.shape[1]), bf16)], axis=0)
+        return mean, squares
+
+    def lines(row_of_all):
+        return jnp.concatenate([row_of_all[:, k * 128 : (k + 1) * 128] for k in range(8)], axis=0)
 
     def share_copy(d, part, got, send, recv):
         there = (x + d) % X
@@ -126,22 +124,54 @@
 
     share_t = lambda d: share_copy(d, part_t, got_t, rst_s, rst_r)
     share_i = lambda d: share_copy(d, part_i, got_i, rsi_s, rsi_r)
+
+    def stat_copy(d):
+        return remote(stats.at[x], stats.at[x], stat_s.at[d], stat_r.at[d], mp=(x + d) % X)
+
+    mean_t, squares_t = centred(ft, gt, lhs_t)
     loads_p[0].wait()
-    value = dot(normed(ft[...].astype(f32), 2, f32(X * ft.shape[1]), gain_t[...]), pt[...])
-    own_t[...] = value
-    part_t[...] = value.astype(bf16)
-    each(1, X, lambda d: share_t(d).start())
+    value = dot(lhs_t[...], pt[...])
+    own_t[...] = value[:HALF]
+    part_t[...] = value[:HALF].astype(bf16)
+    stats[x, 16:] = lines(value[HALF : HALF + 1] + value[HALF + 1 : HALF + 2])
+    mean_i, squares_i = centred(fi, gi, lhs_i)
+    packed = jnp.where(lane == 0, mean_i, 0.0)
+    packed = jnp.where(lane == 1, squares_i, packed)
+    packed = jnp.where(lane == 2, mean_t, packed)
+    packed = jnp.where(lane == 3, squares_t, packed)
+    stats[x, :8] = packed.T[:8]
+    pl.semaphore_wait(barrier, XY - 1 + ZC - 1)
+    for d in (2, 1, 3):
+        share_t(d).start()
     loads_p[1].wait()
-    value = dot(normed(fi[...].astype(f32), 0, f32(X * fi.shape[1]), gain_i[...]), pi[...])
-    own_i[...] = value
-    part_i[...] = value.astype(bf16)
-    each(1, X, lambda d: share_i(d).start())
-
-    def unit_of(own, got):
+    value = dot(lhs_i[...], pi[...])
+    own_i[...] = value[:HALF]
+    part_i[...] = value[:HALF].astype(bf16)
+    stats[x, 8:16] = lines(value[HALF : HALF + 1] + value[HALF + 1 : HALF + 2])
+    for d in (2, 1, 3):
+        stat_copy(d).start()
+    for d in (2, 1, 3):
+        share_i(d).start()
+
+    each(1, X, lambda d: stat_copy(d).wait_recv())
+    turned = jnp.concatenate([stats[k, :8] for k in range(X)] + [jnp.zeros((96, 128), f32)], axis=0).T
+    moments[...] = turned
+    moment = moments[pl.ds(pl.multiple_of(x * PIECE, PIECE), PIECE)]
+
+    def unit_of(own, got, which, width):
+        means = [moment[:, 8 * k + 2 * which : 8 * k + 2 * which + 1] for k in range(X)]
+        squares = [moment[:, 8 * k + 2 * which + 1 : 8 * k + 2 * which + 2] for k in range(X)]
+        average = (means[0] + means[1] + means[2] + means[3]) * (1.0 / X)
+        spread = (squares[0] + squares[1] + squares[2] + squares[3]) / width - average * average
         value = own[pl.ds(pl.multiple_of(x * PIECE, PIECE), PIECE)]
         for d in range(1, X):
             value = value + got[d].astype(f32)
-        return (value * lax.rsqrt(jnp.sum(value * value, axis=1, keepdims=True) + 1e-06)).astype(bf16)
+        for k in range(X):
+            gained = stats[k, 8 * (1 + which) : 8 * (2 + which)]
+            gained = jnp.concatenate([gained[q : q + 1] for q in range(8)], axis=1)
+            value = value + (means[k] - average) * gained
+        size = jnp.sum(value * value, axis=1, keepdims=True) + 1e-06 * (spread + epsilon)
+        return (value * lax.rsqrt(size)).astype(bf16)
 
     def slot(buffer, index):
         return buffer.at[pl.ds(pl.multiple_of(index * PIECE, PIECE), PIECE)]
@@ -159,10 +189,10 @@
         return remote(held, held, fwd_s.at[d], fwd_r.at[d], dp_2=1 - c)
 
     each(1, X, lambda d: share_t(d).wait_recv())
-    tbuf[pl.ds(pl.multiple_of(xy * PIECE, PIECE), PIECE)] = unit_of(own_t, got_t)
+    tbuf[pl.ds(pl.multiple_of(xy * PIECE, PIECE), PIECE)] = unit_of(own_t, got_t, 1, f32(X * ft.shape[1]))
     each(1, XY, lambda d: text_copy(d).start())
     each(1, X, lambda d: share_i(d).wait_recv())
-    ibuf[pl.ds(pl.multiple_of(zc * PIECE, PIECE), PIECE)] = unit_of(own_i, got_i)
+    ibuf[pl.ds(pl.multiple_of(zc * PIECE, PIECE), PIECE)] = unit_of(own_i, got_i, 0, f32(X * fi.shape[1]))
     each(1, Z, lambda d: image_copy(d).start())
     forward(0).start()
     for d in (1, 7, 2, 6, 3, 5, 4):
@@ -210,6 +240,7 @@
         peak = jnp.max(values, axis=0)
         return peak + jnp.log(jnp.sum(jnp.exp(values - peak[None]), axis=0))
 
+    load_pair.wait()
     held = pair[pl.ds(y * 16 + x // 2, 8, stride=2), :]
     held = jnp.where(x % 2 == 1, pltpu.roll(held, 64, 1), held)
     held = jnp.concatenate([held] * 16, axis=0).T
@@ -230,7 +261,6 @@
         target = target + jnp.sum(flags * s, axis=0, keepdims=True)
         w = scale * (jnp.exp(s - turned[:, k : k + 1]) + jnp.exp(s - line_c) - 2.0 * flags)
         weights[rows] = w.astype(bf16)
-    row = lax.broadcasted_iota(jnp.int32, (8, 128), 0)
     shared = jnp.where(row < 4, total_r + total_c, 0.0) * (1.0 / 16)
     loss_1[zc] = shared - 2.0 * as_tile(target)
 
@@ -348,14 +378,20 @@
             jax.ShapeDtypeStruct((1, ROWS, emb), f32),
             jax.ShapeDtypeStruct((1, 1), f32),
         ),
-        in_specs=[hbm, hbm, vmem, vmem, hbm, hbm, vmem, smem],
+        in_specs=[hbm, hbm, hbm, hbm, hbm, hbm, hbm, smem],
         out_specs=(vmem, smem),
         scratch_shapes=[
             pltpu.VMEM((HALF, width_i), bf16),
             pltpu.VMEM((HALF, width_t), bf16),
+            pltpu.VMEM((width_i // 128, 128), f32),
+            pltpu.VMEM((width_t // 128, 128), f32),
+            pltpu.VMEM((pair.size // 128, 128), jnp.int32),
             pltpu.VMEM((width_i, emb), bf16),
             pltpu.VMEM((width_t, emb), bf16),
-            pltpu.VMEM((X, 8, 128), f32),
+            pltpu.VMEM((HALF + 16, width_i), bf16),
+            pltpu.VMEM((HALF + 16, width_t), bf16),
+            pltpu.VMEM((X, 24, 128), f32),
+            pltpu.VMEM((128, 128), f32),
             pltpu.VMEM((HALF, emb), bf16),
             pltpu.VMEM((HALF, emb), bf16),
             pltpu.VMEM((HALF, emb), f32),
@@ -379,7 +415,7 @@
             pltpu.VMEM((XY, PIECE, emb), bf16),
             pltpu.VMEM((PIECE, emb), bf16),
             pltpu.VMEM((PIECE, emb), bf16),
-            dma(2 * X + 2),
+            dma(2 * X + 5),
             dma(X), dma(X), dma(X), dma(X), dma(X), dma(X),
             dma(Z), dma(Z), dma(Z), dma(Z), dma(XY), dma(XY),
             dma(ZC), dma(ZC), dma(XY), dma(XY), dma(ZC), dma(ZC), dma(XY), dma(XY),
@@ -388,11 +424,11 @@
             pltpu.SemaphoreType.DMA, pltpu.SemaphoreType.DMA,
         ],
         compiler_params=pltpu.CompilerParams(
-            collective_id=0, has_side_effects=True, vmem_limit_bytes=48 * 1024 * 1024
+            collective_id=0, has_side_effects=True, vmem_limit_bytes=67043328
         ),
         name="contrastive",
     )(
-        image_features, text_features, image_gain.reshape(1, -1), text_gain.reshape(1, -1),
+        image_features, text_features, image_gain.reshape(-1, 128), text_gain.reshape(-1, 128),
         image_proj, text_proj, pair.reshape(-1, 128), logit_scale.reshape(1, 1),
     )
     return grads, loss.reshape(())

time: 82.4 us -> 73.1 us (0.89)
  local copies, waits for them, and re-layouts: 7.81 us -> 1.67 us
  Pallas kernels: 70.6 us -> 68.3 us
    unnamed x13 -> x1, local copies, waits for them, and re-layouts: 7.11 us -> 1.67 us
    pallas_call x1, Pallas kernels: 70.6 us -> 68.3 us  [body(): pl.pallas_call(kernel, out_shape=(jax.ShapeDtypeStruct((1, ROWS, emb), f3...]
where the time goes in v2:
time: 73.1 us; the launch traced here: 73 us
  Pallas kernels  68.3 us (93%)
  between operations  3.05 us (4%)
  local copies, waits for them, and re-layouts  1.67 us (2%)
    pallas_call x1, Pallas kernels, body(): pl.pallas_call(kernel, out_shape=(jax.ShapeDtypeStruct((1, ROWS, emb), f3...  68.3 us
    unnamed x1, local copies, waits for them, and re-layouts  1.67 us

profile of v2, /device:TPU:1, one launch (start us, length us, event | category | flops | bytes accessed | tf_op | source)
XLA Modules:
  0.0 73.0 jit_solution(10580306767223271856)
XLA Ops:
  1.3 68.3 %contrastive.1 = (f32[1,64,1024]{2,1,0:T(8,128)}, f32[1,1]{1,0:T(1,128)}) custom-call(bf16[256,1536]{1,0:T(8,128)(2,1)} %feat_i.1, bf16[256,256]{1,0:T(8,128)(2,1)} %feat_t.1, f32[12,128]{1,0:T(8,128)} %bitcast.7, f32[2,128]{1,0:T(2,128)} %bitcast.8, bf16[1536,1024]{1,0:T(8,128)(2,1)} %proj_i.1, bf16[256,1024]{1,0:T(8,128)(2,1)} %proj_t.1, ...), custom_call_target="tpu_custom_call" | custom-call | tf_op jit(solution)/shard_map/contrastive/pallas_call | solution.py:375
  69.5 1.7 %copy.13 = f32[1,64,1024]{2,1,0:T(8,128)} copy(f32[1,64,1024]{2,1,0:T(8,128)} %get-tuple-element.8) | data formatting | bytes 524288

commit v3 on v2

--- a/solution.py
+++ b/solution.py
@@ -20,6 +20,7 @@
 HALF = X * PIECE
 BLOCK = XY * PIECE
 ROWS = 2 * PIECE
+HALF_E = 512
 SIDE = Z * PIECE
 
 epsilon = 1e-05
@@ -29,6 +30,15 @@
 
 def dot(a, b, dims=((1,), (0,))):
     return lax.dot_general(a, b, (dims, ((), ())), preferred_element_type=f32)
+
+
+def hops(d, size):
+    return min(d, size - d)
+
+
+PLANE = sorted(range(1, XY), key=lambda d: -hops(d % X, X) - hops(d // X, Y))
+COLUMN = sorted(range(1, ZC), key=lambda d: -hops(d % Z, Z))
+RING = (2, 1, 3)
 
 
 def each(low, high, step):
@@ -44,11 +54,12 @@
     out, loss_out,
     fi, ft, gi, gt, pair, pi, pt, lhs_i, lhs_t, stats, moments, part_i, part_t, own_i, own_t, got_i, got_t,
     ibuf, tbuf, scores, weights, lse_r, lse_c, loss_1, loss_2,
-    img_d2d, img_d2d_got, img_send, img_own, img_got, txt_send, txt_got, fin, fin_got,
+    img_d2d, img_d2d_got, img_send, img_own, img_got,
+    txt_send, sum_x, sum_y, sent_x, sent_y, sum_xy, sum_yx, fin, fin_got,
     load_sem, stat_s, stat_r, rsi_s, rsi_r, rst_s, rst_r,
-    agi_s, agi_r, fwd_s, fwd_r, agt_s, agt_r,
+    agi_s, agi_r, agh_s, agh_r, fwd_s, fwd_r, agx_s, agx_r, agy_s, agy_r, axy_s, axy_r, ayx_s, ayx_r,
     lr_s, lr_r, lc_s, lc_r, l1_s, l1_r, l2_s, l2_r,
-    d2d_s, d2d_r, gi_s, gi_r, gt_s, gt_r, fin_s, fin_r,
+    d2d_s, d2d_r, gi_s, gi_r, gx_s, gx_r, gy_s, gy_r, gxy_s, gxy_r, gyx_s, gyx_r, fin_s, fin_r,
 ):
     x, y = lax.axis_index("mp"), lax.axis_index("dp_0")
     zh, c, zl = lax.axis_index("dp_1"), lax.axis_index("dp_2"), lax.axis_index("group")
@@ -176,13 +187,40 @@
     def slot(buffer, index):
         return buffer.at[pl.ds(pl.multiple_of(index * PIECE, PIECE), PIECE)]
 
-    def text_copy(d):
+    def half(buffer, index, which):
+        return buffer.at[pl.ds(pl.multiple_of(index * PIECE + which * (PIECE // 2), 16), PIECE // 2)]
+
+    def text_x(d):
         mine = slot(tbuf, xy)
-        return remote(mine, mine, agt_s.at[d], agt_r.at[d], **plane(d))
+        return remote(mine, mine, agx_s.at[d], agx_r.at[d], mp=(x + d) % X)
+
+    def text_y(d):
+        mine = slot(tbuf, xy)
+        return remote(mine, mine, agy_s.at[d], agy_r.at[d], dp_0=(y + d) % Y)
+
+    def text_xy(d, e):
+        held = half(tbuf, y * X + (x + X - d) % X, 0)
+        return remote(held, held, axy_s.at[d * 4 + e], axy_r.at[d * 4 + e], dp_0=(y + e) % Y)
+
+    def text_yx(d, e):
+        held = half(tbuf, (y + Y - d) % Y * X + x, 1)
+        return remote(held, held, ayx_s.at[d * 4 + e], ayx_r.at[d * 4 + e], mp=(x + e) % X)
+
+    def along(d):
+        there = (z + d) % Z
+        return {"dp_1": there // ZL, "group": there % ZL}
 
     def image_copy(d):
         mine = slot(ibuf, zc)
-        return remote(mine, mine, agi_s.at[d], agi_r.at[d], **column(d))
+        return remote(mine, mine, agi_s.at[d], agi_r.at[d], **along(d))
+
+    def image_on(d):
+        held = slot(ibuf, c * Z + (z + Z - (2 if d == 3 else 6)) % Z)
+        return remote(held, held, agi_s.at[d], agi_r.at[d], **along(1 if d == 3 else 7))
+
+    def image_half(which):
+        held = half(ibuf, c * Z + (z + Z - (2, 6)[which]) % Z, which)
+        return remote(held, held, agh_s.at[which], agh_r.at[which], **along((2, 6)[which]))
 
     def forward(d):
         held = slot(ibuf, c * Z + (z + Z - d) % Z)
@@ -190,16 +228,40 @@
 
     each(1, X, lambda d: share_t(d).wait_recv())
     tbuf[pl.ds(pl.multiple_of(xy * PIECE, PIECE), PIECE)] = unit_of(own_t, got_t, 1, f32(X * ft.shape[1]))
-    each(1, XY, lambda d: text_copy(d).start())
+    for d in RING:
+        text_x(d).start()
+        text_y(d).start()
     each(1, X, lambda d: share_i(d).wait_recv())
     ibuf[pl.ds(pl.multiple_of(zc * PIECE, PIECE), PIECE)] = unit_of(own_i, got_i, 0, f32(X * fi.shape[1]))
-    each(1, Z, lambda d: image_copy(d).start())
+    for d in (2, 6, 1, 7):
+        image_copy(d).start()
     forward(0).start()
-    for d in (1, 7, 2, 6, 3, 5, 4):
+    for d in (1, 3, 2):
+        text_x(d).wait_recv()
+        for e in RING:
+            text_xy(d, e).start()
+        text_y(d).wait_recv()
+        for e in RING:
+            text_yx(d, e).start()
+    for d in (2, 6):
+        image_copy(d).wait_recv()
+        image_half(0 if d == 2 else 1).start()
+        image_on(3 if d == 2 else 5).start()
+        forward(d).start()
+    for d in (1, 7):
         image_copy(d).wait_recv()
         forward(d).start()
+    for d in (3, 5):
+        image_on(d).wait_recv()
+        forward(d).start()
+    image_half(0).wait_recv()
+    image_half(1).wait_recv()
+    forward(4).start()
+    for d in range(1, X):
+        for e in range(1, X):
+            text_xy(d, e).wait_recv()
+            text_yx(d, e).wait_recv()
     each(0, Z, lambda d: forward(d).wait_recv())
-    each(1, XY, lambda d: text_copy(d).wait_recv())
 
     scale = scale_ref[0, 0]
     quarters = [pl.ds(k * 128, 128) for k in range(BLOCK // 128)]
@@ -221,7 +283,8 @@
     def lse_c_copy(d):
         return remote(lse_c.at[xy], lse_c.at[xy], lc_s.at[d], lc_r.at[d], **plane(d))
 
-    each(1, ZC, lambda d: lse_r_copy(d).start())
+    for d in COLUMN:
+        lse_r_copy(d).start()
     sum_c = jnp.zeros((1, BLOCK), f32)
     for rows in quarters:
         sum_c = sum_c + jnp.sum(jnp.exp(scores[rows] - peak_c), axis=0, keepdims=True)
@@ -233,7 +296,8 @@
         )
 
     lse_c[xy] = as_tile(log_sum)
-    each(1, XY, lambda d: lse_c_copy(d).start())
+    for d in PLANE:
+        lse_c_copy(d).start()
 
     def combined(parts):
         values = parts[...]
@@ -270,22 +334,42 @@
     def loss_2_copy(d):
         return remote(loss_2.at[xy], loss_2.at[xy], l2_s.at[d], l2_r.at[d], **plane(d))
 
-    each(1, ZC, lambda d: loss_1_copy(d).start())
+    for d in COLUMN:
+        loss_1_copy(d).start()
 
     d2d = remote(img_d2d, img_d2d_got, d2d_s, d2d_r, dp_2=1 - c)
     rows = pl.ds(pl.multiple_of((1 - c) * SIDE, SIDE), SIDE)
     img_d2d[...] = dot(weights[rows], tbuf[...]).astype(bf16)
     d2d.start()
 
-    def grad_t_copy(d):
-        there = plane(d)
-        piece = slot(txt_send, there["dp_0"] * X + there["mp"])
-        return remote(piece, txt_got.at[d], gt_s.at[d], gt_r.at[d], **there)
+    def grad_x(d):
+        there = (x + d) % X
+        return remote(txt_send.at[:, there, :, :HALF_E], sum_x.at[d], gx_s.at[d], gx_r.at[d], mp=there)
+
+    def grad_y(d):
+        there = (y + d) % Y
+        return remote(txt_send.at[there, :, :, HALF_E:], sum_y.at[d], gy_s.at[d], gy_r.at[d], dp_0=there)
+
+    def grad_xy(d):
+        there = (y + d) % Y
+        return remote(sent_x.at[there], sum_xy.at[d], gxy_s.at[d], gxy_r.at[d], dp_0=there)
+
+    def grad_yx(d):
+        there = (x + d) % X
+        return remote(sent_y.at[there], sum_yx.at[d], gyx_s.at[d], gyx_r.at[d], mp=there)
 
     for k in range(4):
         cols = pl.ds(k * 128, 128)
-        txt_send[cols] = dot(weights[:, cols], ibuf[...], ((0,), (0,))).astype(bf16)
-    each(1, XY, lambda d: grad_t_copy(d).start())
+        value = dot(weights[:, cols], ibuf[:, :HALF_E], ((0,), (0,)))
+        txt_send[k, :, :, :HALF_E] = value.reshape(X, PIECE, HALF_E).astype(bf16)
+    for d in RING:
+        grad_x(d).start()
+    for k in range(4):
+        cols = pl.ds(k * 128, 128)
+        value = dot(weights[:, cols], ibuf[:, HALF_E:], ((0,), (0,)))
+        txt_send[k, :, :, HALF_E:] = value.reshape(X, PIECE, HALF_E).astype(bf16)
+    for d in RING:
+        grad_y(d).start()
 
     def grad_i_copy(d):
         there = (zh + d) % ZH
@@ -300,26 +384,49 @@
     img_own[...] = value
     img_send[...] = value.astype(bf16)
 
+    for d in (2, 3, 1):
+        grad_i_copy(d).start()
+
     @pl.when(zl == 1)
     def _():
         grad_i_copy(0).start()
 
-    each(1, ZH, lambda d: grad_i_copy(d).start())
-
     each(1, ZC, lambda d: loss_1_copy(d).wait_recv())
     loss_2[xy] = jnp.sum(loss_1[...], axis=0)
-    each(1, XY, lambda d: loss_2_copy(d).start())
-
-    each(1, XY, lambda d: grad_t_copy(d).wait_recv())
-    value = txt_send[pl.ds(pl.multiple_of(xy * PIECE, PIECE), PIECE)].astype(f32)
-    for d in range(1, XY):
-        value = value + txt_got[d].astype(f32)
+    for d in PLANE:
+        loss_2_copy(d).start()
+
+    each(1, X, lambda d: grad_x(d).wait_recv())
+    for k in range(Y):
+        value = txt_send[k, x, :, :HALF_E].astype(f32)
+        for d in range(1, X):
+            value = value + sum_x[d, k].astype(f32)
+        sent_x[k] = value.astype(bf16)
+    for d in RING:
+        grad_xy(d).start()
+    each(1, Y, lambda d: grad_y(d).wait_recv())
+    for k in range(X):
+        value = txt_send[y, k, :, HALF_E:].astype(f32)
+        for d in range(1, Y):
+            value = value + sum_y[d, k].astype(f32)
+        sent_y[k] = value.astype(bf16)
+    for d in RING:
+        grad_yx(d).start()
+    each(1, Y, lambda d: grad_xy(d).wait_recv())
+    first = sent_x[y].astype(f32)
+    for d in range(1, Y):
+        first = first + sum_xy[d].astype(f32)
+    each(1, X, lambda d: grad_yx(d).wait_recv())
+    second = sent_y[x].astype(f32)
+    for d in range(1, X):
+        second = second + sum_yx[d].astype(f32)
 
     last = remote(fin, fin_got, fin_s, fin_r, group=1)
 
     @pl.when(zl == 0)
     def _():
-        fin[...] = value.astype(bf16)
+        fin[:, :HALF_E] = first.astype(bf16)
+        fin[:, HALF_E:] = second.astype(bf16)
         last.start()
         own = img_own[pl.ds(pl.multiple_of(zh * ROWS, ROWS), ROWS)]
 
@@ -334,7 +441,8 @@
 
     @pl.when(zl == 1)
     def _():
-        out[0, PIECE:] = value
+        out[0, PIECE:, :HALF_E] = first
+        out[0, PIECE:, HALF_E:] = second
         grad_i_copy(0).wait_send()
         last.wait_recv()
         out[0, :PIECE] = fin_got[...].astype(f32)
@@ -342,24 +450,36 @@
     each(1, XY, lambda d: loss_2_copy(d).wait_recv())
     loss_out[0, 0] = jnp.sum(jnp.sum(loss_2[...], axis=0)) * (1.0 / (2 * XY * BLOCK))
 
-    def sent_x(d):
+    def sent_ring(d):
         stat_copy(d).wait_send()
         share_t(d).wait_send()
         share_i(d).wait_send()
         grad_i_copy(d).wait_send()
-
-    def sent_plane(d):
-        text_copy(d).wait_send()
+        text_x(d).wait_send()
+        text_y(d).wait_send()
+        grad_x(d).wait_send()
+        grad_y(d).wait_send()
+        grad_xy(d).wait_send()
+        grad_yx(d).wait_send()
+        for e in range(1, X):
+            text_xy(d, e).wait_send()
+            text_yx(d, e).wait_send()
+
+    def sent_all(d):
         lse_r_copy(d).wait_send()
         lse_c_copy(d).wait_send()
         loss_1_copy(d).wait_send()
         loss_2_copy(d).wait_send()
-        grad_t_copy(d).wait_send()
-
-    each(1, X, sent_x)
-    each(1, Z, lambda d: image_copy(d).wait_send())
+
+    each(1, X, sent_ring)
+    for d in (1, 2, 6, 7):
+        image_copy(d).wait_send()
+    image_on(3).wait_send()
+    image_on(5).wait_send()
+    image_half(0).wait_send()
+    image_half(1).wait_send()
     each(0, Z, lambda d: forward(d).wait_send())
-    each(1, XY, sent_plane)
+    each(1, XY, sent_all)
     d2d.wait_send()
 
 
@@ -411,16 +531,22 @@
             pltpu.VMEM((SIDE, emb), bf16),
             pltpu.VMEM((SIDE, emb), f32),
             pltpu.VMEM((Z, ROWS, emb), bf16),
-            pltpu.VMEM((BLOCK, emb), bf16),
-            pltpu.VMEM((XY, PIECE, emb), bf16),
+            pltpu.VMEM((Y, X, PIECE, emb), bf16),
+            pltpu.VMEM((X, Y, PIECE, HALF_E), bf16),
+            pltpu.VMEM((Y, X, PIECE, HALF_E), bf16),
+            pltpu.VMEM((Y, PIECE, HALF_E), bf16),
+            pltpu.VMEM((X, PIECE, HALF_E), bf16),
+            pltpu.VMEM((Y, PIECE, HALF_E), bf16),
+            pltpu.VMEM((X, PIECE, HALF_E), bf16),
             pltpu.VMEM((PIECE, emb), bf16),
             pltpu.VMEM((PIECE, emb), bf16),
             dma(2 * X + 5),
             dma(X), dma(X), dma(X), dma(X), dma(X), dma(X),
-            dma(Z), dma(Z), dma(Z), dma(Z), dma(XY), dma(XY),
+            dma(Z), dma(Z), dma(2), dma(2), dma(Z), dma(Z), dma(X), dma(X), dma(Y), dma(Y),
+            dma(XY), dma(XY), dma(XY), dma(XY),
             dma(ZC), dma(ZC), dma(XY), dma(XY), dma(ZC), dma(ZC), dma(XY), dma(XY),
             pltpu.SemaphoreType.DMA, pltpu.SemaphoreType.DMA,
-            dma(ZH), dma(Z), dma(XY), dma(XY),
+            dma(ZH), dma(Z), dma(X), dma(X), dma(Y), dma(Y), dma(Y), dma(Y), dma(X), dma(X),
             pltpu.SemaphoreType.DMA, pltpu.SemaphoreType.DMA,
         ],
         compiler_params=pltpu.CompilerParams(

time: 73.1 us -> 69.1 us (0.945)
  Pallas kernels: 68.3 us -> 64.2 us
    pallas_call x1, Pallas kernels: 68.3 us -> 64.2 us  [body(): pl.pallas_call(kernel, out_shape=(jax.ShapeDtypeStruct((1, ROWS, emb), f3...]
where the time goes in v3:
time: 69.1 us; the launch traced here: 68.9 us
  Pallas kernels  64.2 us (93%)
  between operations  3.05 us (4%)
  local copies, waits for them, and re-layouts  1.67 us (2%)
    pallas_call x1, Pallas kernels, body(): pl.pallas_call(kernel, out_shape=(jax.ShapeDtypeStruct((1, ROWS, emb), f3...  64.2 us
    unnamed x1, local copies, waits for them, and re-layouts  1.67 us

profile of v3, /device:TPU:1, one launch (start us, length us, event | category | flops | bytes accessed | tf_op | source)
XLA Modules:
  0.0 68.9 jit_solution(7469600825583048303)
XLA Ops:
  1.3 64.2 %contrastive.1 = (f32[1,64,1024]{2,1,0:T(8,128)}, f32[1,1]{1,0:T(1,128)}) custom-call(bf16[256,1536]{1,0:T(8,128)(2,1)} %feat_i.1, bf16[256,256]{1,0:T(8,128)(2,1)} %feat_t.1, f32[12,128]{1,0:T(8,128)} %bitcast.7, f32[2,128]{1,0:T(2,128)} %bitcast.8, bf16[1536,1024]{1,0:T(8,128)(2,1)} %proj_i.1, bf16[256,1024]{1,0:T(8,128)(2,1)} %proj_t.1, ...), custom_call_target="tpu_custom_call" | custom-call | tf_op jit(solution)/shard_map/contrastive/pallas_call | solution.py:495
  65.5 1.7 %copy.13 = f32[1,64,1024]{2,1,0:T(8,128)} copy(f32[1,64,1024]{2,1,0:T(8,128)} %get-tuple-element.8) | data formatting | bytes 524288

commit v4 on v3

--- a/solution.py
+++ b/solution.py
@@ -54,12 +54,12 @@
     out, loss_out,
     fi, ft, gi, gt, pair, pi, pt, lhs_i, lhs_t, stats, moments, part_i, part_t, own_i, own_t, got_i, got_t,
     ibuf, tbuf, scores, weights, lse_r, lse_c, loss_1, loss_2,
-    img_d2d, img_d2d_got, img_send, img_own, img_got,
+    img_d2d, img_d2d_got, img_send, img_near, img_third_got, img_fourth_got, img_sum, img_far,
     txt_send, sum_x, sum_y, sent_x, sent_y, sum_xy, sum_yx, fin, fin_got,
     load_sem, stat_s, stat_r, rsi_s, rsi_r, rst_s, rst_r,
     agi_s, agi_r, agh_s, agh_r, fwd_s, fwd_r, agx_s, agx_r, agy_s, agy_r, axy_s, axy_r, ayx_s, ayx_r,
     lr_s, lr_r, lc_s, lc_r, l1_s, l1_r, l2_s, l2_r,
-    d2d_s, d2d_r, gi_s, gi_r, gx_s, gx_r, gy_s, gy_r, gxy_s, gxy_r, gyx_s, gyx_r, fin_s, fin_r,
+    d2d_s, d2d_r, in_s, in_r, i3_s, i3_r, i4_s, i4_r, if_s, if_r, gx_s, gx_r, gy_s, gy_r, gxy_s, gxy_r, gyx_s, gyx_r, fin_s, fin_r,
 ):
     x, y = lax.axis_index("mp"), lax.axis_index("dp_0")
     zh, c, zl = lax.axis_index("dp_1"), lax.axis_index("dp_2"), lax.axis_index("group")
@@ -80,22 +80,20 @@
         there = (z + d % Z) % Z
         return {"dp_1": there // ZL, "group": there % ZL, "dp_2": (c + d // Z) % C}
 
-    loads = []
+    loads_i, loads_t = [], []
     for k in range(X):
         rows = pl.ds(pl.multiple_of(k * ROWS + zl * PIECE, PIECE), PIECE)
         here = pl.ds(k * PIECE, PIECE)
-        loads.append(pltpu.make_async_copy(feat_i.at[rows], fi.at[here], load_sem.at[k]))
-        loads.append(pltpu.make_async_copy(feat_t.at[rows], ft.at[here], load_sem.at[X + k]))
-    loads += [
-        pltpu.make_async_copy(gain_i, gi, load_sem.at[2 * X + 2]),
-        pltpu.make_async_copy(gain_t, gt, load_sem.at[2 * X + 3]),
-    ]
+        loads_i.append(pltpu.make_async_copy(feat_i.at[rows], fi.at[here], load_sem.at[k]))
+        loads_t.append(pltpu.make_async_copy(feat_t.at[rows], ft.at[here], load_sem.at[X + k]))
+    loads_i.append(pltpu.make_async_copy(gain_i, gi, load_sem.at[2 * X + 2]))
+    loads_t.append(pltpu.make_async_copy(gain_t, gt, load_sem.at[2 * X + 3]))
     loads_p = [
         pltpu.make_async_copy(proj_t, pt, load_sem.at[2 * X]),
         pltpu.make_async_copy(proj_i, pi, load_sem.at[2 * X + 1]),
     ]
     load_pair = pltpu.make_async_copy(pair_hbm, pair, load_sem.at[2 * X + 4])
-    for copy in loads + loads_p + [load_pair]:
+    for copy in loads_t + loads_p[:1] + loads_i + loads_p[1:] + [load_pair]:
         copy.start()
 
     barrier = pltpu.get_barrier_semaphore()
@@ -109,10 +107,7 @@
     each(1, XY, greet_plane)
     each(1, ZC, greet_column)
 
-    for copy in loads:
-        copy.wait()
     lane = lax.broadcasted_iota(jnp.int32, (HALF, 128), 1)
-    row = lax.broadcasted_iota(jnp.int32, (8, 128), 0)
 
     def centred(features, gain, lhs):
         values = features[...].astype(f32)
@@ -139,21 +134,25 @@
     def stat_copy(d):
         return remote(stats.at[x], stats.at[x], stat_s.at[d], stat_r.at[d], mp=(x + d) % X)
 
+    for copy in loads_t:
+        copy.wait()
     mean_t, squares_t = centred(ft, gt, lhs_t)
     loads_p[0].wait()
     value = dot(lhs_t[...], pt[...])
     own_t[...] = value[:HALF]
     part_t[...] = value[:HALF].astype(bf16)
+    pl.semaphore_wait(barrier, XY - 1 + ZC - 1)
+    for d in (2, 1, 3):
+        share_t(d).start()
     stats[x, 16:] = lines(value[HALF : HALF + 1] + value[HALF + 1 : HALF + 2])
+    for copy in loads_i:
+        copy.wait()
     mean_i, squares_i = centred(fi, gi, lhs_i)
     packed = jnp.where(lane == 0, mean_i, 0.0)
     packed = jnp.where(lane == 1, squares_i, packed)
     packed = jnp.where(lane == 2, mean_t, packed)
     packed = jnp.where(lane == 3, squares_t, packed)
     stats[x, :8] = packed.T[:8]
-    pl.semaphore_wait(barrier, XY - 1 + ZC - 1)
-    for d in (2, 1, 3):
-        share_t(d).start()
     loads_p[1].wait()
     value = dot(lhs_i[...], pi[...])
     own_i[...] = value[:HALF]
@@ -275,7 +274,7 @@
         packed = jnp.where(lane == k, log_sum, packed)
         high = jnp.max(s, axis=0, keepdims=True)
         peak_c = high if peak_c is None else jnp.maximum(peak_c, high)
-    lse_r[zc] = packed.T[:8]
+    lse_r[zc] = packed.T[:4]
 
     def lse_r_copy(d):
         return remote(lse_r.at[zc], lse_r.at[zc], lr_s.at[d], lr_r.at[d], **column(d))
@@ -292,7 +291,7 @@
 
     def as_tile(line):
         return jnp.concatenate(
-            [line[:, k * 128 : (k + 1) * 128] for k in range(4)] + [jnp.zeros((4, 128), f32)], axis=0
+            [line[:, k * 128 : (k + 1) * 128] for k in range(4)], axis=0
         )
 
     lse_c[xy] = as_tile(log_sum)
@@ -314,7 +313,7 @@
 
     each(1, ZC, lambda d: lse_r_copy(d).wait_recv())
     total_r = combined(lse_r)
-    turned = jnp.concatenate([total_r] * 16, axis=0).T
+    turned = jnp.concatenate([total_r] * 32, axis=0).T
     each(1, XY, lambda d: lse_c_copy(d).wait_recv())
     total_c = combined(lse_c)
     line_c = jnp.concatenate([total_c[k : k + 1] for k in range(4)], axis=1)
@@ -325,7 +324,7 @@
         target = target + jnp.sum(flags * s, axis=0, keepdims=True)
         w = scale * (jnp.exp(s - turned[:, k : k + 1]) + jnp.exp(s - line_c) - 2.0 * flags)
         weights[rows] = w.astype(bf16)
-    shared = jnp.where(row < 4, total_r + total_c, 0.0) * (1.0 / 16)
+    shared = (total_r + total_c) * (1.0 / 16)
     loss_1[zc] = shared - 2.0 * as_tile(target)
 
     def loss_1_copy(d):
@@ -364,6 +363,32 @@
         txt_send[k, :, :, :HALF_E] = value.reshape(X, PIECE, HALF_E).astype(bf16)
     for d in RING:
         grad_x(d).start()
+    def piece(index):
+        return img_send.at[pl.ds(pl.multiple_of((z + index) % Z * PIECE, PIECE), PIECE)]
+
+    def img_next(side):
+        return remote(piece((1, 7)[side]), img_near.at[side], in_s.at[side], in_r.at[side], **along((1, 7)[side]))
+
+    def img_third(side):
+        return remote(piece((3, 5)[side]), img_third_got.at[side], i3_s.at[side], i3_r.at[side], **along((1, 7)[side]))
+
+    def img_fourth(side):
+        start = (z + 4) % Z * PIECE + side * (PIECE // 2)
+        part = img_send.at[pl.ds(pl.multiple_of(start, 16), PIECE // 2)]
+        return remote(part, img_fourth_got.at[side], i4_s.at[side], i4_r.at[side], **along((2, 6)[side]))
+
+    def img_second(side):
+        return remote(img_sum.at[side], img_far.at[side], if_s.at[side], if_r.at[side], **along((2, 6)[side]))
+
+    rows = pl.ds(pl.multiple_of(c * SIDE, SIDE), SIDE)
+    value = dot(weights[rows], tbuf[...])
+    d2d.wait_recv()
+    value = value + img_d2d_got[...].astype(f32)
+    img_send[...] = value.astype(bf16)
+    for send in (img_fourth, img_third, img_next):
+        send(0).start()
+        send(1).start()
+
     for k in range(4):
         cols = pl.ds(k * 128, 128)
         value = dot(weights[:, cols], ibuf[:, HALF_E:], ((0,), (0,)))
@@ -371,30 +396,24 @@
     for d in RING:
         grad_y(d).start()
 
-    def grad_i_copy(d):
-        there = (zh + d) % ZH
-        piece = img_send.at[pl.ds(pl.multiple_of(there * ROWS, ROWS), ROWS)]
-        gap = (there * ZL + Z - z) % Z
-        return remote(piece, img_got.at[gap], gi_s.at[d], gi_r.at[gap], dp_1=there, group=0)
-
-    rows = pl.ds(pl.multiple_of(c * SIDE, SIDE), SIDE)
-    value = dot(weights[rows], tbuf[...])
-    d2d.wait_recv()
-    value = value + img_d2d_got[...].astype(f32)
-    img_own[...] = value
-    img_send[...] = value.astype(bf16)
-
-    for d in (2, 3, 1):
-        grad_i_copy(d).start()
-
-    @pl.when(zl == 1)
-    def _():
-        grad_i_copy(0).start()
-
     each(1, ZC, lambda d: loss_1_copy(d).wait_recv())
     loss_2[xy] = jnp.sum(loss_1[...], axis=0)
     for d in PLANE:
         loss_2_copy(d).start()
+
+    def image_rows(index, start, count):
+        return img_send[pl.ds(pl.multiple_of((z + index) % Z * PIECE + start, 16), count)].astype(f32)
+
+    for side in range(2):
+        img_fourth(side).wait_recv()
+        img_third(side).wait_recv()
+        for part in range(2):
+            rows = pl.ds(part * (PIECE // 2), PIECE // 2)
+            value = image_rows((2, 6)[side], part * (PIECE // 2), PIECE // 2) + img_third_got[side, rows].astype(f32)
+            if part == side:
+                value = value + img_fourth_got[side].astype(f32)
+            img_sum[side, rows] = value.astype(bf16)
+        img_second(side).start()
 
     each(1, X, lambda d: grad_x(d).wait_recv())
     for k in range(Y):
@@ -421,29 +440,37 @@
     for d in range(1, X):
         second = second + sum_yx[d].astype(f32)
 
-    last = remote(fin, fin_got, fin_s, fin_r, group=1)
+    last = remote(fin, fin_got, fin_s, fin_r, group=1 - zl)
 
     @pl.when(zl == 0)
     def _():
         fin[:, :HALF_E] = first.astype(bf16)
         fin[:, HALF_E:] = second.astype(bf16)
         last.start()
-        own = img_own[pl.ds(pl.multiple_of(zh * ROWS, ROWS), ROWS)]
-
-        def arrived(gap):
-            remote(img_send.at[:ROWS], img_got.at[gap], gi_s.at[0], gi_r.at[gap], group=0).wait_recv()
-
-        each(1, Z, arrived)
-        for gap in range(1, Z):
-            own = own + img_got[gap].astype(f32)
-        out[0] = own
-        last.wait_send()
 
     @pl.when(zl == 1)
     def _():
         out[0, PIECE:, :HALF_E] = first
         out[0, PIECE:, HALF_E:] = second
-        grad_i_copy(0).wait_send()
+
+    third = image_rows(0, 0, PIECE)
+    for side in range(2):
+        img_next(side).wait_recv()
+        third = third + img_near[side].astype(f32)
+    for side in range(2):
+        img_second(side).wait_recv()
+        third = third + img_far[side].astype(f32)
+
+    @pl.when(zl == 0)
+    def _():
+        out[0, :PIECE] = third
+        last.wait_recv()
+        out[0, PIECE:] = fin_got[...].astype(f32)
+
+    @pl.when(zl == 1)
+    def _():
+        fin[...] = third.astype(bf16)
+        last.start()
         last.wait_recv()
         out[0, :PIECE] = fin_got[...].astype(f32)
 
@@ -454,7 +481,6 @@
         stat_copy(d).wait_send()
         share_t(d).wait_send()
         share_i(d).wait_send()
-        grad_i_copy(d).wait_send()
         text_x(d).wait_send()
         text_y(d).wait_send()
         grad_x(d).wait_send()
@@ -480,6 +506,12 @@
     image_half(1).wait_send()
     each(0, Z, lambda d: forward(d).wait_send())
     each(1, XY, sent_all)
+    for side in range(2):
+        img_next(side).wait_send()
+        img_third(side).wait_send()
+        img_fourth(side).wait_send()
+        img_second(side).wait_send()
+    last.wait_send()
     d2d.wait_send()
 
 
@@ -522,15 +554,18 @@
             pltpu.VMEM((BLOCK, emb), bf16),
             pltpu.VMEM((BLOCK, BLOCK), f32),
             pltpu.VMEM((BLOCK, BLOCK), bf16),
-            pltpu.VMEM((ZC, 8, 128), f32),
-            pltpu.VMEM((XY, 8, 128), f32),
-            pltpu.VMEM((ZC, 8, 128), f32),
-            pltpu.VMEM((XY, 8, 128), f32),
+            pltpu.VMEM((ZC, 4, 128), f32),
+            pltpu.VMEM((XY, 4, 128), f32),
+            pltpu.VMEM((ZC, 4, 128), f32),
+            pltpu.VMEM((XY, 4, 128), f32),
             pltpu.VMEM((SIDE, emb), bf16),
             pltpu.VMEM((SIDE, emb), bf16),
             pltpu.VMEM((SIDE, emb), bf16),
-            pltpu.VMEM((SIDE, emb), f32),
-            pltpu.VMEM((Z, ROWS, emb), bf16),
+            pltpu.VMEM((2, PIECE, emb), bf16),
+            pltpu.VMEM((2, PIECE, emb), bf16),
+            pltpu.VMEM((2, PIECE // 2, emb), bf16),
+            pltpu.VMEM((2, PIECE, emb), bf16),
+            pltpu.VMEM((2, PIECE, emb), bf16),
             pltpu.VMEM((Y, X, PIECE, emb), bf16),
             pltpu.VMEM((X, Y, PIECE, HALF_E), bf16),
             pltpu.VMEM((Y, X, PIECE, HALF_E), bf16),
@@ -546,7 +581,8 @@
             dma(XY), dma(XY), dma(XY), dma(XY),
             dma(ZC), dma(ZC), dma(XY), dma(XY), dma(ZC), dma(ZC), dma(XY), dma(XY),
             pltpu.SemaphoreType.DMA, pltpu.SemaphoreType.DMA,
-            dma(ZH), dma(Z), dma(X), dma(X), dma(Y), dma(Y), dma(Y), dma(Y), dma(X), dma(X),
+            dma(2), dma(2), dma(2), dma(2), dma(2), dma(2), dma(2), dma(2),
+            dma(X), dma(X), dma(Y), dma(Y), dma(Y), dma(Y), dma(X), dma(X),
             pltpu.SemaphoreType.DMA, pltpu.SemaphoreType.DMA,
         ],
         compiler_params=pltpu.CompilerParams(

time: 69.1 us -> 64.8 us (0.938)
  Pallas kernels: 64.2 us -> 59.5 us
    pallas_call x1, Pallas kernels: 64.2 us -> 59.5 us  [body(): pl.pallas_call(kernel, out_shape=(jax.ShapeDtypeStruct((1, ROWS, emb), f3...]
where the time goes in v4:
time: 64.8 us; the launch traced here: 64.2 us
  Pallas kernels  59.5 us (92%)
  between operations  3.05 us (5%)
  local copies, waits for them, and re-layouts  1.67 us (3%)
    pallas_call x1, Pallas kernels, body(): pl.pallas_call(kernel, out_shape=(jax.ShapeDtypeStruct((1, ROWS, emb), f3...  59.5 us
    unnamed x1, local copies, waits for them, and re-layouts  1.67 us

profile of v4, /device:TPU:1, one launch (start us, length us, event | category | flops | bytes accessed | tf_op | source)
XLA Modules:
  0.0 64.2 jit_solution(15490621986043342772)
XLA Ops:
  1.3 59.5 %contrastive.1 = (f32[1,64,1024]{2,1,0:T(8,128)}, f32[1,1]{1,0:T(1,128)}) custom-call(bf16[256,1536]{1,0:T(8,128)(2,1)} %feat_i.1, bf16[256,256]{1,0:T(8,128)(2,1)} %feat_t.1, f32[12,128]{1,0:T(8,128)} %bitcast.7, f32[2,128]{1,0:T(2,128)} %bitcast.8, bf16[1536,1024]{1,0:T(8,128)(2,1)} %proj_i.1, bf16[256,1024]{1,0:T(8,128)(2,1)} %proj_t.1, ...), custom_call_target="tpu_custom_call" | custom-call | tf_op jit(solution)/shard_map/contrastive/pallas_call | solution.py:527
  60.8 1.7 %copy.13 = f32[1,64,1024]{2,1,0:T(8,128)} copy(f32[1,64,1024]{2,1,0:T(8,128)} %get-tuple-element.8) | data formatting | bytes 524288

commit v5 on v4

--- a/solution.py
+++ b/solution.py
@@ -50,13 +50,13 @@
 
 
 def kernel(
-    feat_i, feat_t, gain_i, gain_t, proj_i, proj_t, pair_hbm, scale_ref,
+    feat_i, feat_t, gain_i, gain_t, proj_i, proj_t, pair_hbm, scale_hbm,
     out, loss_out,
-    fi, ft, gi, gt, pair, pi, pt, lhs_i, lhs_t, stats, moments, part_i, part_t, own_i, own_t, got_i, got_t,
+    scale_ref, result, loss_ref, fi, ft, gi, gt, pair, pi, pt, lhs_i, lhs_t, stats, moments, part_i, part_t, own_i, own_t, got_i, got_t,
     ibuf, tbuf, scores, weights, lse_r, lse_c, loss_1, loss_2,
     img_d2d, img_d2d_got, img_send, img_near, img_third_got, img_fourth_got, img_sum, img_far,
     txt_send, sum_x, sum_y, sent_x, sent_y, sum_xy, sum_yx, fin, fin_got,
-    load_sem, stat_s, stat_r, rsi_s, rsi_r, rst_s, rst_r,
+    load_sem, store_sem, stat_s, stat_r, rsi_s, rsi_r, rst_s, rst_r,
     agi_s, agi_r, agh_s, agh_r, fwd_s, fwd_r, agx_s, agx_r, agy_s, agy_r, axy_s, axy_r, ayx_s, ayx_r,
     lr_s, lr_r, lc_s, lc_r, l1_s, l1_r, l2_s, l2_r,
     d2d_s, d2d_r, in_s, in_r, i3_s, i3_r, i4_s, i4_r, if_s, if_r, gx_s, gx_r, gy_s, gy_r, gxy_s, gxy_r, gyx_s, gyx_r, fin_s, fin_r,
@@ -93,7 +93,8 @@
         pltpu.make_async_copy(proj_i, pi, load_sem.at[2 * X + 1]),
     ]
     load_pair = pltpu.make_async_copy(pair_hbm, pair, load_sem.at[2 * X + 4])
-    for copy in loads_t + loads_p[:1] + loads_i + loads_p[1:] + [load_pair]:
+    load_scale = pltpu.make_async_copy(scale_hbm, scale_ref, load_sem.at[2 * X + 5])
+    for copy in loads_t + loads_p[:1] + loads_i + loads_p[1:] + [load_pair, load_scale]:
         copy.start()
 
     barrier = pltpu.get_barrier_semaphore()
@@ -262,7 +263,8 @@
             text_yx(d, e).wait_recv()
     each(0, Z, lambda d: forward(d).wait_recv())
 
-    scale = scale_ref[0, 0]
+    load_scale.wait()
+    scale = scale_ref[...]
     quarters = [pl.ds(k * 128, 128) for k in range(BLOCK // 128)]
     packed = jnp.zeros((128, 128), f32)
     peak_c = None
@@ -336,11 +338,6 @@
     for d in COLUMN:
         loss_1_copy(d).start()
 
-    d2d = remote(img_d2d, img_d2d_got, d2d_s, d2d_r, dp_2=1 - c)
-    rows = pl.ds(pl.multiple_of((1 - c) * SIDE, SIDE), SIDE)
-    img_d2d[...] = dot(weights[rows], tbuf[...]).astype(bf16)
-    d2d.start()
-
     def grad_x(d):
         there = (x + d) % X
         return remote(txt_send.at[:, there, :, :HALF_E], sum_x.at[d], gx_s.at[d], gx_r.at[d], mp=there)
@@ -363,6 +360,18 @@
         txt_send[k, :, :, :HALF_E] = value.reshape(X, PIECE, HALF_E).astype(bf16)
     for d in RING:
         grad_x(d).start()
+    d2d = remote(img_d2d, img_d2d_got, d2d_s, d2d_r, dp_2=1 - c)
+    rows = pl.ds(pl.multiple_of((1 - c) * SIDE, SIDE), SIDE)
+    img_d2d[...] = dot(weights[rows], tbuf[...]).astype(bf16)
+    d2d.start()
+
+    for k in range(4):
+        cols = pl.ds(k * 128, 128)
+        value = dot(weights[:, cols], ibuf[:, HALF_E:], ((0,), (0,)))
+        txt_send[k, :, :, HALF_E:] = value.reshape(X, PIECE, HALF_E).astype(bf16)
+    for d in RING:
+        grad_y(d).start()
+
     def piece(index):
         return img_send.at[pl.ds(pl.multiple_of((z + index) % Z * PIECE, PIECE), PIECE)]
 
@@ -388,13 +397,6 @@
     for send in (img_fourth, img_third, img_next):
         send(0).start()
         send(1).start()
-
-    for k in range(4):
-        cols = pl.ds(k * 128, 128)
-        value = dot(weights[:, cols], ibuf[:, HALF_E:], ((0,), (0,)))
-        txt_send[k, :, :, HALF_E:] = value.reshape(X, PIECE, HALF_E).astype(bf16)
-    for d in RING:
-        grad_y(d).start()
 
     each(1, ZC, lambda d: loss_1_copy(d).wait_recv())
     loss_2[xy] = jnp.sum(loss_1[...], axis=0)
@@ -431,51 +433,66 @@
         sent_y[k] = value.astype(bf16)
     for d in RING:
         grad_yx(d).start()
+    def last(part):
+        cols = pl.ds(part * HALF_E, HALF_E)
+        return remote(fin.at[:, cols], fin_got.at[:, cols], fin_s.at[part], fin_r.at[part], group=1 - zl)
+
+    mine = pl.ds(pl.multiple_of(zl * PIECE, PIECE), PIECE)
+    theirs = pl.ds(pl.multiple_of((1 - zl) * PIECE, PIECE), PIECE)
+    store = pltpu.make_async_copy(result.at[mine], out.at[0, mine], store_sem.at[0])
+    store_theirs = pltpu.make_async_copy(result.at[theirs], out.at[0, theirs], store_sem.at[1])
+
+    def finished_text(part, value):
+        cols = pl.ds(part * HALF_E, HALF_E)
+
+        @pl.when(zl == 0)
+        def _():
+            fin[:, cols] = value.astype(bf16)
+            last(part).start()
+
+        @pl.when(zl == 1)
+        def _():
+            result[PIECE:, cols] = value
+
     each(1, Y, lambda d: grad_xy(d).wait_recv())
-    first = sent_x[y].astype(f32)
+    value = sent_x[y].astype(f32)
     for d in range(1, Y):
-        first = first + sum_xy[d].astype(f32)
+        value = value + sum_xy[d].astype(f32)
+    finished_text(0, value)
     each(1, X, lambda d: grad_yx(d).wait_recv())
-    second = sent_y[x].astype(f32)
+    value = sent_y[x].astype(f32)
     for d in range(1, X):
-        second = second + sum_yx[d].astype(f32)
-
-    last = remote(fin, fin_got, fin_s, fin_r, group=1 - zl)
+        value = value + sum_yx[d].astype(f32)
+    finished_text(1, value)
+
+    value = image_rows(0, 0, PIECE)
+    for side in range(2):
+        img_next(side).wait_recv()
+        value = value + img_near[side].astype(f32)
+    for side in range(2):
+        img_second(side).wait_recv()
+        value = value + img_far[side].astype(f32)
 
     @pl.when(zl == 0)
     def _():
-        fin[:, :HALF_E] = first.astype(bf16)
-        fin[:, HALF_E:] = second.astype(bf16)
-        last.start()
+        result[:PIECE] = value
 
     @pl.when(zl == 1)
     def _():
-        out[0, PIECE:, :HALF_E] = first
-        out[0, PIECE:, HALF_E:] = second
-
-    third = image_rows(0, 0, PIECE)
-    for side in range(2):
-        img_next(side).wait_recv()
-        third = third + img_near[side].astype(f32)
-    for side in range(2):
-        img_second(side).wait_recv()
-        third = third + img_far[side].astype(f32)
-
-    @pl.when(zl == 0)
-    def _():
-        out[0, :PIECE] = third
-        last.wait_recv()
-        out[0, PIECE:] = fin_got[...].astype(f32)
-
-    @pl.when(zl == 1)
-    def _():
-        fin[...] = third.astype(bf16)
-        last.start()
-        last.wait_recv()
-        out[0, :PIECE] = fin_got[...].astype(f32)
-
+        fin[...] = value.astype(bf16)
+        last(0).start()
+        last(1).start()
+
+    store.start()
     each(1, XY, lambda d: loss_2_copy(d).wait_recv())
-    loss_out[0, 0] = jnp.sum(jnp.sum(loss_2[...], axis=0)) * (1.0 / (2 * XY * BLOCK))
+    total = jnp.sum(jnp.sum(loss_2[...], axis=0), axis=0, keepdims=True)
+    loss_ref[...] = jnp.sum(total, axis=1, keepdims=True) * (1.0 / (2 * XY * BLOCK))
+    store_loss = pltpu.make_async_copy(loss_ref, loss_out, store_sem.at[2])
+    store_loss.start()
+    last(0).wait_recv()
+    last(1).wait_recv()
+    result[theirs] = fin_got[...].astype(f32)
+    store_theirs.start()
 
     def sent_ring(d):
         stat_copy(d).wait_send()
@@ -511,8 +528,12 @@
         img_third(side).wait_send()
         img_fourth(side).wait_send()
         img_second(side).wait_send()
-    last.wait_send()
+    last(0).wait_send()
+    last(1).wait_send()
     d2d.wait_send()
+    store.wait()
+    store_loss.wait()
+    store_theirs.wait()
 
 
 def body(
@@ -520,8 +541,6 @@
 ):
     width_i, width_t = image_features.shape[1], text_features.shape[1]
     emb = image_proj.shape[1]
-    vmem = pl.BlockSpec(memory_space=pltpu.VMEM)
-    smem = pl.BlockSpec(memory_space=pltpu.SMEM)
     hbm = pl.BlockSpec(memory_space=pl.ANY)
     dma = lambda *n: pltpu.SemaphoreType.DMA(n)
     grads, loss = pl.pallas_call(
@@ -530,9 +549,12 @@
             jax.ShapeDtypeStruct((1, ROWS, emb), f32),
             jax.ShapeDtypeStruct((1, 1), f32),
         ),
-        in_specs=[hbm, hbm, hbm, hbm, hbm, hbm, hbm, smem],
-        out_specs=(vmem, smem),
+        in_specs=[hbm] * 8,
+        out_specs=(hbm, hbm),
         scratch_shapes=[
+            pltpu.VMEM((1, 1), f32),
+            pltpu.VMEM((ROWS, emb), f32),
+            pltpu.VMEM((1, 1), f32),
             pltpu.VMEM((HALF, width_i), bf16),
             pltpu.VMEM((HALF, width_t), bf16),
             pltpu.VMEM((width_i // 128, 128), f32),
@@ -575,7 +597,7 @@
             pltpu.VMEM((X, PIECE, HALF_E), bf16),
             pltpu.VMEM((PIECE, emb), bf16),
             pltpu.VMEM((PIECE, emb), bf16),
-            dma(2 * X + 5),
+            dma(2 * X + 6), dma(3),
             dma(X), dma(X), dma(X), dma(X), dma(X), dma(X),
             dma(Z), dma(Z), dma(2), dma(2), dma(Z), dma(Z), dma(X), dma(X), dma(Y), dma(Y),
             dma(XY), dma(XY), dma(XY), dma(XY),
@@ -583,7 +605,7 @@
             pltpu.SemaphoreType.DMA, pltpu.SemaphoreType.DMA,
             dma(2), dma(2), dma(2), dma(2), dma(2), dma(2), dma(2), dma(2),
             dma(X), dma(X), dma(Y), dma(Y), dma(Y), dma(Y), dma(X), dma(X),
-            pltpu.SemaphoreType.DMA, pltpu.SemaphoreType.DMA,
+            dma(2), dma(2),
         ],
         compiler_params=pltpu.CompilerParams(
             collective_id=0, has_side_effects=True, vmem_limit_bytes=67043328

time: 64.8 us -> 62.1 us (0.958)
  Pallas kernels: 59.5 us -> 56.9 us
    pallas_call x1, Pallas kernels: 59.5 us -> 56.9 us  [body(): pl.pallas_call(kernel, out_shape=(jax.ShapeDtypeStruct((1, ROWS, emb), f3...]
where the time goes in v5:
time: 62.1 us; the launch traced here: 61.6 us
  Pallas kernels  56.9 us (92%)
  between operations  3.05 us (5%)
  local copies, waits for them, and re-layouts  1.67 us (3%)
    pallas_call x1, Pallas kernels, body(): pl.pallas_call(kernel, out_shape=(jax.ShapeDtypeStruct((1, ROWS, emb), f3...  56.9 us
    unnamed x1, local copies, waits for them, and re-layouts  1.67 us

profile of v5, /device:TPU:1, one launch (start us, length us, event | category | flops | bytes accessed | tf_op | source)
XLA Modules:
  0.0 61.6 jit_solution(12900238352098294824)
XLA Ops:
  1.3 56.9 %contrastive.1 = (f32[1,64,1024]{2,1,0:T(8,128)}, f32[1,1]{1,0:T(1,128)}) custom-call(bf16[256,1536]{1,0:T(8,128)(2,1)} %feat_i.1, bf16[256,256]{1,0:T(8,128)(2,1)} %feat_t.1, f32[12,128]{1,0:T(8,128)} %bitcast.7, f32[2,128]{1,0:T(2,128)} %bitcast.8, bf16[1536,1024]{1,0:T(8,128)(2,1)} %proj_i.1, bf16[256,1024]{1,0:T(8,128)(2,1)} %proj_t.1, ...), custom_call_target="tpu_custom_call" | custom-call | tf_op jit(solution)/shard_map/contrastive/pallas_call | solution.py:546
  58.1 1.7 %copy.13 = f32[1,64,1024]{2,1,0:T(8,128)} copy(f32[1,64,1024]{2,1,0:T(8,128)} %get-tuple-element.8) | data formatting | bytes 524288

commit v6 on v5

--- a/solution.py
+++ b/solution.py
@@ -94,7 +94,7 @@
     ]
     load_pair = pltpu.make_async_copy(pair_hbm, pair, load_sem.at[2 * X + 4])
     load_scale = pltpu.make_async_copy(scale_hbm, scale_ref, load_sem.at[2 * X + 5])
-    for copy in loads_t + loads_p[:1] + loads_i + loads_p[1:] + [load_pair, load_scale]:
+    for copy in loads_i + loads_p[1:] + loads_t + loads_p[:1] + [load_pair, load_scale]:
         copy.start()
 
     barrier = pltpu.get_barrier_semaphore()
@@ -105,8 +105,10 @@
     def greet_column(d):
         pl.semaphore_signal(barrier, inc=1, device_id=column(d), device_id_type=MESH)
 
-    each(1, XY, greet_plane)
-    each(1, ZC, greet_column)
+    for d in PLANE:
+        greet_plane(d)
+    for d in COLUMN:
+        greet_column(d)
 
     lane = lax.broadcasted_iota(jnp.int32, (HALF, 128), 1)
 
@@ -135,34 +137,34 @@
     def stat_copy(d):
         return remote(stats.at[x], stats.at[x], stat_s.at[d], stat_r.at[d], mp=(x + d) % X)
 
+    for copy in loads_i:
+        copy.wait()
+    mean_i, squares_i = centred(fi, gi, lhs_i)
+    loads_p[1].wait()
+    value = dot(lhs_i[...], pi[...])
+    own_i[...] = value[:HALF]
+    part_i[...] = value[:HALF].astype(bf16)
+    pl.semaphore_wait(barrier, XY - 1 + ZC - 1)
+    for d in RING:
+        share_i(d).start()
+    stats[x, 8:16] = lines(value[HALF : HALF + 1] + value[HALF + 1 : HALF + 2])
     for copy in loads_t:
         copy.wait()
     mean_t, squares_t = centred(ft, gt, lhs_t)
-    loads_p[0].wait()
-    value = dot(lhs_t[...], pt[...])
-    own_t[...] = value[:HALF]
-    part_t[...] = value[:HALF].astype(bf16)
-    pl.semaphore_wait(barrier, XY - 1 + ZC - 1)
-    for d in (2, 1, 3):
-        share_t(d).start()
-    stats[x, 16:] = lines(value[HALF : HALF + 1] + value[HALF + 1 : HALF + 2])
-    for copy in loads_i:
-        copy.wait()
-    mean_i, squares_i = centred(fi, gi, lhs_i)
     packed = jnp.where(lane == 0, mean_i, 0.0)
     packed = jnp.where(lane == 1, squares_i, packed)
     packed = jnp.where(lane == 2, mean_t, packed)
     packed = jnp.where(lane == 3, squares_t, packed)
     stats[x, :8] = packed.T[:8]
-    loads_p[1].wait()
-    value = dot(lhs_i[...], pi[...])
-    own_i[...] = value[:HALF]
-    part_i[...] = value[:HALF].astype(bf16)
-    stats[x, 8:16] = lines(value[HALF : HALF + 1] + value[HALF + 1 : HALF + 2])
-    for d in (2, 1, 3):
+    loads_p[0].wait()
+    value = dot(lhs_t[...], pt[...])
+    own_t[...] = value[:HALF]
+    part_t[...] = value[:HALF].astype(bf16)
+    stats[x, 16:] = lines(value[HALF : HALF + 1] + value[HALF + 1 : HALF + 2])
+    for d in RING:
         stat_copy(d).start()
-    for d in (2, 1, 3):
-        share_i(d).start()
+    for d in RING:
+        share_t(d).start()
 
     each(1, X, lambda d: stat_copy(d).wait_recv())
     turned = jnp.concatenate([stats[k, :8] for k in range(X)] + [jnp.zeros((96, 128), f32)], axis=0).T
@@ -226,31 +228,38 @@
         held = slot(ibuf, c * Z + (z + Z - d) % Z)
         return remote(held, held, fwd_s.at[d], fwd_r.at[d], dp_2=1 - c)
 
-    each(1, X, lambda d: share_t(d).wait_recv())
-    tbuf[pl.ds(pl.multiple_of(xy * PIECE, PIECE), PIECE)] = unit_of(own_t, got_t, 1, f32(X * ft.shape[1]))
-    for d in RING:
-        text_x(d).start()
-        text_y(d).start()
     each(1, X, lambda d: share_i(d).wait_recv())
     ibuf[pl.ds(pl.multiple_of(zc * PIECE, PIECE), PIECE)] = unit_of(own_i, got_i, 0, f32(X * fi.shape[1]))
     for d in (2, 6, 1, 7):
         image_copy(d).start()
     forward(0).start()
+    each(1, X, lambda d: share_t(d).wait_recv())
+    tbuf[pl.ds(pl.multiple_of(xy * PIECE, PIECE), PIECE)] = unit_of(own_t, got_t, 1, f32(X * ft.shape[1]))
     for d in (1, 3, 2):
+        text_x(d).start()
+        text_y(d).start()
+    for d in (2, 6):
+        image_copy(d).wait_recv()
+        image_half(0 if d == 2 else 1).start()
+        image_on(3 if d == 2 else 5).start()
+        forward(d).start()
+    for d in (1, 3):
         text_x(d).wait_recv()
         for e in RING:
             text_xy(d, e).start()
         text_y(d).wait_recv()
         for e in RING:
             text_yx(d, e).start()
-    for d in (2, 6):
-        image_copy(d).wait_recv()
-        image_half(0 if d == 2 else 1).start()
-        image_on(3 if d == 2 else 5).start()
-        forward(d).start()
     for d in (1, 7):
         image_copy(d).wait_recv()
         forward(d).start()
+    for d in (2,):
+        text_x(d).wait_recv()
+        for e in RING:
+            text_xy(d, e).start()
+        text_y(d).wait_recv()
+        for e in RING:
+            text_yx(d, e).start()
     for d in (3, 5):
         image_on(d).wait_recv()
         forward(d).start()
@@ -261,21 +270,29 @@
         for e in range(1, X):
             text_xy(d, e).wait_recv()
             text_yx(d, e).wait_recv()
-    each(0, Z, lambda d: forward(d).wait_recv())
 
     load_scale.wait()
     scale = scale_ref[...]
     quarters = [pl.ds(k * 128, 128) for k in range(BLOCK // 128)]
     packed = jnp.zeros((128, 128), f32)
-    peak_c = None
-    for k, rows in enumerate(quarters):
+    for turn in range(4):
+        quarter = (c if turn < 2 else 1 - c) * 2 + turn % 2
+        rows = pl.ds(pl.multiple_of(quarter * 128, 128), 128)
+        if turn == 2:
+            each(0, Z, lambda d: forward(d).wait_recv())
         s = scale * dot(ibuf[rows], tbuf[...], ((1,), (1,)))
         scores[rows] = s
         peak = jnp.max(s, axis=1, keepdims=True)
         log_sum = peak + jnp.log(jnp.sum(jnp.exp(s - peak), axis=1, keepdims=True))
-        packed = jnp.where(lane == k, log_sum, packed)
+        packed = jnp.where(lane == quarter, log_sum, packed)
         high = jnp.max(s, axis=0, keepdims=True)
-        peak_c = high if peak_c is None else jnp.maximum(peak_c, high)
+        if turn == 0:
+            peak_c = high
+            sum_c = jnp.sum(jnp.exp(s - high), axis=0, keepdims=True)
+        else:
+            high = jnp.maximum(high, peak_c)
+            sum_c = sum_c * jnp.exp(peak_c - high) + jnp.sum(jnp.exp(s - high), axis=0, keepdims=True)
+            peak_c = high
     lse_r[zc] = packed.T[:4]
 
     def lse_r_copy(d):
@@ -286,9 +303,6 @@
 
     for d in COLUMN:
         lse_r_copy(d).start()
-    sum_c = jnp.zeros((1, BLOCK), f32)
-    for rows in quarters:
-        sum_c = sum_c + jnp.sum(jnp.exp(scores[rows] - peak_c), axis=0, keepdims=True)
     log_sum = peak_c + jnp.log(sum_c)
 
     def as_tile(line):
@@ -402,6 +416,32 @@
     loss_2[xy] = jnp.sum(loss_1[...], axis=0)
     for d in PLANE:
         loss_2_copy(d).start()
+
+    def sent_ring(d):
+        stat_copy(d).wait_send()
+        share_t(d).wait_send()
+        share_i(d).wait_send()
+        text_x(d).wait_send()
+        text_y(d).wait_send()
+        for e in range(1, X):
+            text_xy(d, e).wait_send()
+            text_yx(d, e).wait_send()
+
+    def sent_all(d):
+        lse_r_copy(d).wait_send()
+        lse_c_copy(d).wait_send()
+        loss_1_copy(d).wait_send()
+
+    each(1, X, sent_ring)
+    for d in (1, 2, 6, 7):
+        image_copy(d).wait_send()
+    image_on(3).wait_send()
+    image_on(5).wait_send()
+    image_half(0).wait_send()
+    image_half(1).wait_send()
+    each(0, Z, lambda d: forward(d).wait_send())
+    each(1, XY, sent_all)
+    d2d.wait_send()
 
     def image_rows(index, start, count):
         return img_send[pl.ds(pl.multiple_of((z + index) % Z * PIECE + start, 16), count)].astype(f32)
@@ -484,6 +524,12 @@
         last(1).start()
 
     store.start()
+    for side in range(2):
+        img_next(side).wait_send()
+        img_third(side).wait_send()
+        img_fourth(side).wait_send()
+    each(1, X, lambda d: grad_x(d).wait_send())
+    each(1, X, lambda d: grad_y(d).wait_send())
     each(1, XY, lambda d: loss_2_copy(d).wait_recv())
     total = jnp.sum(jnp.sum(loss_2[...], axis=0), axis=0, keepdims=True)
     loss_ref[...] = jnp.sum(total, axis=1, keepdims=True) * (1.0 / (2 * XY * BLOCK))
@@ -494,43 +540,12 @@
     result[theirs] = fin_got[...].astype(f32)
     store_theirs.start()
 
-    def sent_ring(d):
-        stat_copy(d).wait_send()
-        share_t(d).wait_send()
-        share_i(d).wait_send()
-        text_x(d).wait_send()
-        text_y(d).wait_send()
-        grad_x(d).wait_send()
-        grad_y(d).wait_send()
-        grad_xy(d).wait_send()
-        grad_yx(d).wait_send()
-        for e in range(1, X):
-            text_xy(d, e).wait_send()
-            text_yx(d, e).wait_send()
-
-    def sent_all(d):
-        lse_r_copy(d).wait_send()
-        lse_c_copy(d).wait_send()
-        loss_1_copy(d).wait_send()
-        loss_2_copy(d).wait_send()
-
-    each(1, X, sent_ring)
-    for d in (1, 2, 6, 7):
-        image_copy(d).wait_send()
-    image_on(3).wait_send()
-    image_on(5).wait_send()
-    image_half(0).wait_send()
-    image_half(1).wait_send()
-    each(0, Z, lambda d: forward(d).wait_send())
-    each(1, XY, sent_all)
+    each(1, XY, lambda d: loss_2_copy(d).wait_send())
+    each(1, X, lambda d: grad_xy(d).wait_send())
+    each(1, X, lambda d: grad_yx(d).wait_send())
     for side in range(2):
-        img_next(side).wait_send()
-        img_third(side).wait_send()
-        img_fourth(side).wait_send()
         img_second(side).wait_send()
-    last(0).wait_send()
-    last(1).wait_send()
-    d2d.wait_send()
+        last(side).wait_send()
     store.wait()
     store_loss.wait()
     store_theirs.wait()

time: 62.1 us -> 61 us (0.982)
  Pallas kernels: 56.9 us -> 56.2 us
    pallas_call x1, Pallas kernels: 56.9 us -> 56.2 us  [body(): pl.pallas_call(kernel, out_shape=(jax.ShapeDtypeStruct((1, ROWS, emb), f3...]
where the time goes in v6:
time: 61 us; the launch traced here: 60.9 us
  Pallas kernels  56.2 us (92%)
  between operations  3.05 us (5%)
  local copies, waits for them, and re-layouts  1.67 us (3%)
    pallas_call x1, Pallas kernels, body(): pl.pallas_call(kernel, out_shape=(jax.ShapeDtypeStruct((1, ROWS, emb), f3...  56.2 us
    unnamed x1, local copies, waits for them, and re-layouts  1.67 us

profile of v6, /device:TPU:1, one launch (start us, length us, event | category | flops | bytes accessed | tf_op | source)
XLA Modules:
  0.0 60.9 jit_solution(7180093246130332804)
XLA Ops:
  1.3 56.2 %contrastive.1 = (f32[1,64,1024]{2,1,0:T(8,128)}, f32[1,1]{1,0:T(1,128)}) custom-call(bf16[256,1536]{1,0:T(8,128)(2,1)} %feat_i.1, bf16[256,256]{1,0:T(8,128)(2,1)} %feat_t.1, f32[12,128]{1,0:T(8,128)} %bitcast.7, f32[2,128]{1,0:T(2,128)} %bitcast.8, bf16[1536,1024]{1,0:T(8,128)(2,1)} %proj_i.1, bf16[256,1024]{1,0:T(8,128)(2,1)} %proj_t.1, ...), custom_call_target="tpu_custom_call" | custom-call | tf_op jit(solution)/shard_map/contrastive/pallas_call | solution.py:561
  57.5 1.7 %copy.13 = f32[1,64,1024]{2,1,0:T(8,128)} copy(f32[1,64,1024]{2,1,0:T(8,128)} %get-tuple-element.8) | data formatting | bytes 524288

commit v7 on v6

--- a/solution.py
+++ b/solution.py
@@ -51,11 +51,11 @@
 
 def kernel(
     feat_i, feat_t, gain_i, gain_t, proj_i, proj_t, pair_hbm, scale_hbm,
-    out, loss_out,
-    scale_ref, result, loss_ref, fi, ft, gi, gt, pair, pi, pt, lhs_i, lhs_t, stats, moments, part_i, part_t, own_i, own_t, got_i, got_t,
+    out, out_got, loss_out,
+    scale_ref, blank, result, loss_ref, fi, ft, gi, gt, pair, pi, pt, lhs_i, lhs_t, stats, moments, part_i, part_t, own_i, own_t, got_i, got_t,
     ibuf, tbuf, scores, weights, lse_r, lse_c, loss_1, loss_2,
     img_d2d, img_d2d_got, img_send, img_near, img_third_got, img_fourth_got, img_sum, img_far,
-    txt_send, sum_x, sum_y, sent_x, sent_y, sum_xy, sum_yx, fin, fin_got,
+    txt_a, txt_b, sum_x, sum_y, sent_x, sent_y, sum_xy, sum_yx, fin, fin_got,
     load_sem, store_sem, stat_s, stat_r, rsi_s, rsi_r, rst_s, rst_r,
     agi_s, agi_r, agh_s, agh_r, fwd_s, fwd_r, agx_s, agx_r, agy_s, agy_r, axy_s, axy_r, ayx_s, ayx_r,
     lr_s, lr_r, lc_s, lc_r, l1_s, l1_r, l2_s, l2_r,
@@ -349,16 +349,14 @@
     def loss_2_copy(d):
         return remote(loss_2.at[xy], loss_2.at[xy], l2_s.at[d], l2_r.at[d], **plane(d))
 
-    for d in COLUMN:
-        loss_1_copy(d).start()
 
     def grad_x(d):
         there = (x + d) % X
-        return remote(txt_send.at[:, there, :, :HALF_E], sum_x.at[d], gx_s.at[d], gx_r.at[d], mp=there)
+        return remote(txt_a.at[there], sum_x.at[d], gx_s.at[d], gx_r.at[d], mp=there)
 
     def grad_y(d):
         there = (y + d) % Y
-        return remote(txt_send.at[there, :, :, HALF_E:], sum_y.at[d], gy_s.at[d], gy_r.at[d], dp_0=there)
+        return remote(txt_b.at[there], sum_y.at[d], gy_s.at[d], gy_r.at[d], dp_0=there)
 
     def grad_xy(d):
         there = (y + d) % Y
@@ -371,18 +369,20 @@
     for k in range(4):
         cols = pl.ds(k * 128, 128)
         value = dot(weights[:, cols], ibuf[:, :HALF_E], ((0,), (0,)))
-        txt_send[k, :, :, :HALF_E] = value.reshape(X, PIECE, HALF_E).astype(bf16)
+        txt_a[:, k] = value.reshape(X, PIECE, HALF_E).astype(bf16)
     for d in RING:
         grad_x(d).start()
     d2d = remote(img_d2d, img_d2d_got, d2d_s, d2d_r, dp_2=1 - c)
     rows = pl.ds(pl.multiple_of((1 - c) * SIDE, SIDE), SIDE)
     img_d2d[...] = dot(weights[rows], tbuf[...]).astype(bf16)
     d2d.start()
+    for d in COLUMN:
+        loss_1_copy(d).start()
 
     for k in range(4):
         cols = pl.ds(k * 128, 128)
         value = dot(weights[:, cols], ibuf[:, HALF_E:], ((0,), (0,)))
-        txt_send[k, :, :, HALF_E:] = value.reshape(X, PIECE, HALF_E).astype(bf16)
+        txt_b[k] = value.reshape(X, PIECE, HALF_E).astype(bf16)
     for d in RING:
         grad_y(d).start()
 
@@ -443,6 +443,19 @@
     each(1, XY, sent_all)
     d2d.wait_send()
 
+    mine = pl.ds(pl.multiple_of(zl * PIECE, PIECE), PIECE)
+    theirs = pl.ds(pl.multiple_of((1 - zl) * PIECE, PIECE), PIECE)
+    store = pltpu.make_async_copy(result.at[mine], out.at[0, mine], store_sem.at[0])
+    store_theirs = pltpu.make_async_copy(fin_got, out_got.at[0, theirs], store_sem.at[1])
+    blank[...] = jnp.zeros_like(blank)
+    result[theirs] = jnp.zeros((PIECE, result.shape[1]), f32)
+    blanks = [
+        pltpu.make_async_copy(blank, out_got.at[0, mine], store_sem.at[3]),
+        pltpu.make_async_copy(result.at[theirs], out.at[0, theirs], store_sem.at[4]),
+    ]
+    for copy in blanks:
+        copy.start()
+
     def image_rows(index, start, count):
         return img_send[pl.ds(pl.multiple_of((z + index) % Z * PIECE + start, 16), count)].astype(f32)
 
@@ -458,29 +471,26 @@
         img_second(side).start()
 
     each(1, X, lambda d: grad_x(d).wait_recv())
-    for k in range(Y):
-        value = txt_send[k, x, :, :HALF_E].astype(f32)
+    for e in RING + (0,):
+        k = (y + e) % Y
+        value = txt_a[x, k].astype(f32)
         for d in range(1, X):
             value = value + sum_x[d, k].astype(f32)
         sent_x[k] = value.astype(bf16)
-    for d in RING:
-        grad_xy(d).start()
+        if e:
+            grad_xy(e).start()
     each(1, Y, lambda d: grad_y(d).wait_recv())
-    for k in range(X):
-        value = txt_send[y, k, :, HALF_E:].astype(f32)
+    for e in RING + (0,):
+        k = (x + e) % X
+        value = txt_b[y, k].astype(f32)
         for d in range(1, Y):
             value = value + sum_y[d, k].astype(f32)
         sent_y[k] = value.astype(bf16)
-    for d in RING:
-        grad_yx(d).start()
+        if e:
+            grad_yx(e).start()
     def last(part):
         cols = pl.ds(part * HALF_E, HALF_E)
         return remote(fin.at[:, cols], fin_got.at[:, cols], fin_s.at[part], fin_r.at[part], group=1 - zl)
-
-    mine = pl.ds(pl.multiple_of(zl * PIECE, PIECE), PIECE)
-    theirs = pl.ds(pl.multiple_of((1 - zl) * PIECE, PIECE), PIECE)
-    store = pltpu.make_async_copy(result.at[mine], out.at[0, mine], store_sem.at[0])
-    store_theirs = pltpu.make_async_copy(result.at[theirs], out.at[0, theirs], store_sem.at[1])
 
     def finished_text(part, value):
         cols = pl.ds(part * HALF_E, HALF_E)
@@ -537,7 +547,6 @@
     store_loss.start()
     last(0).wait_recv()
     last(1).wait_recv()
-    result[theirs] = fin_got[...].astype(f32)
     store_theirs.start()
 
     each(1, XY, lambda d: loss_2_copy(d).wait_send())
@@ -546,6 +555,8 @@
     for side in range(2):
         img_second(side).wait_send()
         last(side).wait_send()
+    for copy in blanks:
+        copy.wait()
     store.wait()
     store_loss.wait()
     store_theirs.wait()
@@ -558,16 +569,18 @@
     emb = image_proj.shape[1]
     hbm = pl.BlockSpec(memory_space=pl.ANY)
     dma = lambda *n: pltpu.SemaphoreType.DMA(n)
-    grads, loss = pl.pallas_call(
+    grads, got, loss = pl.pallas_call(
         kernel,
         out_shape=(
             jax.ShapeDtypeStruct((1, ROWS, emb), f32),
+            jax.ShapeDtypeStruct((1, ROWS, emb), bf16),
             jax.ShapeDtypeStruct((1, 1), f32),
         ),
         in_specs=[hbm] * 8,
-        out_specs=(hbm, hbm),
+        out_specs=(hbm, hbm, hbm),
         scratch_shapes=[
             pltpu.VMEM((1, 1), f32),
+            pltpu.VMEM((PIECE, emb), bf16),
             pltpu.VMEM((ROWS, emb), f32),
             pltpu.VMEM((1, 1), f32),
             pltpu.VMEM((HALF, width_i), bf16),
@@ -603,7 +616,8 @@
             pltpu.VMEM((2, PIECE // 2, emb), bf16),
             pltpu.VMEM((2, PIECE, emb), bf16),
             pltpu.VMEM((2, PIECE, emb), bf16),
-            pltpu.VMEM((Y, X, PIECE, emb), bf16),
+            pltpu.VMEM((X, Y, PIECE, HALF_E), bf16),
+            pltpu.VMEM((Y, X, PIECE, HALF_E), bf16),
             pltpu.VMEM((X, Y, PIECE, HALF_E), bf16),
             pltpu.VMEM((Y, X, PIECE, HALF_E), bf16),
             pltpu.VMEM((Y, PIECE, HALF_E), bf16),
@@ -612,7 +626,7 @@
             pltpu.VMEM((X, PIECE, HALF_E), bf16),
             pltpu.VMEM((PIECE, emb), bf16),
             pltpu.VMEM((PIECE, emb), bf16),
-            dma(2 * X + 6), dma(3),
+            dma(2 * X + 6), dma(5),
             dma(X), dma(X), dma(X), dma(X), dma(X), dma(X),
             dma(Z), dma(Z), dma(2), dma(2), dma(Z), dma(Z), dma(X), dma(X), dma(Y), dma(Y),
             dma(XY), dma(XY), dma(XY), dma(XY),
@@ -630,7 +644,7 @@
         image_features, text_features, image_gain.reshape(-1, 128), text_gain.reshape(-1, 128),
         image_proj, text_proj, pair.reshape(-1, 128), logit_scale.reshape(1, 1),
     )
-    return grads, loss.reshape(())
+    return grads + got.astype(f32), loss.reshape(())
 
 
 def solution(mesh):

time: 61 us -> 60.8 us (level)
  other arithmetic: 0 us -> 1.71 us
  local copies, waits for them, and re-layouts: 1.67 us -> 0 us
    add x0 -> x1, other arithmetic: none -> 1.71 us  [body(): return (grads + got.astype(f32), loss.reshape(()))]
    unnamed x1 -> x0, local copies, waits for them, and re-layouts: 1.67 us -> none
where the time goes in v7:
time: 60.8 us; the launch traced here: 60.7 us
  Pallas kernels  56 us (92%)
  between operations  3.04 us (5%)
  other arithmetic  1.71 us (3%)
    pallas_call x1, Pallas kernels, body(): pl.pallas_call(kernel, out_shape=(jax.ShapeDtypeStruct((1, ROWS, emb), f3...  56 us
    add x1, other arithmetic, body(): return (grads + got.astype(f32), loss.reshape(()))  1.71 us

profile of v7, /device:TPU:1, one launch (start us, length us, event | category | flops | bytes accessed | tf_op | source)
XLA Modules:
  0.0 60.7 jit_solution(15916896747278230978)
XLA Ops:
  1.3 56.0 %contrastive.1 = (f32[1,64,1024]{2,1,0:T(8,128)}, bf16[1,64,1024]{2,1,0:T(8,128)(2,1)}, f32[1,1]{1,0:T(1,128)}) custom-call(bf16[256,1536]{1,0:T(8,128)(2,1)} %feat_i.1, bf16[256,256]{1,0:T(8,128)(2,1)} %feat_t.1, f32[12,128]{1,0:T(8,128)} %bitcast.7, f32[2,128]{1,0:T(2,128)} %bitcast.8, bf16[1536,1024]{1,0:T(8,128)(2,1)} %proj_i.1, ...), custom_call_target="tpu_custom_call" | custom-call | tf_op jit(solution)/shard_map/contrastive/pallas_call | solution.py:572
  57.2 1.7 %convert_add_fusion = f32[1,64,1024]{2,1,0:T(8,128)} fusion(f32[1,64,1024]{2,1,0:T(8,128)} %get-tuple-element.5, bf16[1,64,1024]{2,1,0:T(8,128)(2,1)} %get-tuple-element.6), kind=kLoop, calls=%fused_computation | loop fusion | flops 131072 | bytes 655360 | tf_op jit(solution)/shard_map/add | solution.py:647

commit v8 on v6

--- a/solution.py
+++ b/solution.py
@@ -53,12 +53,12 @@
     feat_i, feat_t, gain_i, gain_t, proj_i, proj_t, pair_hbm, scale_hbm,
     out, loss_out,
     scale_ref, result, loss_ref, fi, ft, gi, gt, pair, pi, pt, lhs_i, lhs_t, stats, moments, part_i, part_t, own_i, own_t, got_i, got_t,
-    ibuf, tbuf, scores, weights, lse_r, lse_c, loss_1, loss_2,
+    ibuf, tbuf, scores, weights, lse_r, lse_c, loss_1, loss_2, loss_3,
     img_d2d, img_d2d_got, img_send, img_near, img_third_got, img_fourth_got, img_sum, img_far,
     txt_send, sum_x, sum_y, sent_x, sent_y, sum_xy, sum_yx, fin, fin_got,
     load_sem, store_sem, stat_s, stat_r, rsi_s, rsi_r, rst_s, rst_r,
     agi_s, agi_r, agh_s, agh_r, fwd_s, fwd_r, agx_s, agx_r, agy_s, agy_r, axy_s, axy_r, ayx_s, ayx_r,
-    lr_s, lr_r, lc_s, lc_r, l1_s, l1_r, l2_s, l2_r,
+    lr_s, lr_r, lc_s, lc_r, l1_s, l1_r, l2_s, l2_r, l3_s, l3_r,
     d2d_s, d2d_r, in_s, in_r, i3_s, i3_r, i4_s, i4_r, if_s, if_r, gx_s, gx_r, gy_s, gy_r, gxy_s, gxy_r, gyx_s, gyx_r, fin_s, fin_r,
 ):
     x, y = lax.axis_index("mp"), lax.axis_index("dp_0")
@@ -327,30 +327,41 @@
     j = lax.broadcasted_iota(jnp.int32, (1, BLOCK), 1)
     ids = ((j // 128) * 8 + zh * C + c) * 256 + ((j // PIECE) % X) * ROWS + zl * PIECE + j % PIECE
 
+    def loss_1_copy(d):
+        return remote(loss_1.at[zc], loss_1.at[zc], l1_s.at[d], l1_r.at[d], **column(d))
+
+    def loss_2_copy(d):
+        return remote(loss_2.at[xy], loss_2.at[xy], l2_s.at[d], l2_r.at[d], **plane(d))
+
+    def loss_3_copy(d):
+        return remote(loss_3.at[zc], loss_3.at[zc], l3_s.at[d], l3_r.at[d], **column(d))
+
+    target = jnp.zeros((1, BLOCK), f32)
+    for k, rows in enumerate(quarters):
+        flags = (captions[k * 128 : (k + 1) * 128] == ids).astype(f32)
+        target = target + jnp.sum(flags * scores[rows], axis=0, keepdims=True)
+    loss_1[zc] = -2.0 * as_tile(target)
+    for d in COLUMN:
+        loss_1_copy(d).start()
+
     each(1, ZC, lambda d: lse_r_copy(d).wait_recv())
     total_r = combined(lse_r)
     turned = jnp.concatenate([total_r] * 32, axis=0).T
     each(1, XY, lambda d: lse_c_copy(d).wait_recv())
     total_c = combined(lse_c)
     line_c = jnp.concatenate([total_c[k : k + 1] for k in range(4)], axis=1)
-    target = jnp.zeros((1, BLOCK), f32)
+    loss_3[zc] = total_c
+    for d in COLUMN:
+        loss_3_copy(d).start()
     for k, rows in enumerate(quarters):
         s = scores[rows]
         flags = (captions[k * 128 : (k + 1) * 128] == ids).astype(f32)
-        target = target + jnp.sum(flags * s, axis=0, keepdims=True)
         w = scale * (jnp.exp(s - turned[:, k : k + 1]) + jnp.exp(s - line_c) - 2.0 * flags)
         weights[rows] = w.astype(bf16)
-    shared = (total_r + total_c) * (1.0 / 16)
-    loss_1[zc] = shared - 2.0 * as_tile(target)
-
-    def loss_1_copy(d):
-        return remote(loss_1.at[zc], loss_1.at[zc], l1_s.at[d], l1_r.at[d], **column(d))
-
-    def loss_2_copy(d):
-        return remote(loss_2.at[xy], loss_2.at[xy], l2_s.at[d], l2_r.at[d], **plane(d))
-
-    for d in COLUMN:
-        loss_1_copy(d).start()
+    each(1, ZC, lambda d: loss_1_copy(d).wait_recv())
+    loss_2[xy] = total_r + jnp.sum(loss_1[...], axis=0)
+    for d in PLANE:
+        loss_2_copy(d).start()
 
     def grad_x(d):
         there = (x + d) % X
@@ -412,11 +423,6 @@
         send(0).start()
         send(1).start()
 
-    each(1, ZC, lambda d: loss_1_copy(d).wait_recv())
-    loss_2[xy] = jnp.sum(loss_1[...], axis=0)
-    for d in PLANE:
-        loss_2_copy(d).start()
-
     def sent_ring(d):
         stat_copy(d).wait_send()
         share_t(d).wait_send()
@@ -431,6 +437,7 @@
         lse_r_copy(d).wait_send()
         lse_c_copy(d).wait_send()
         loss_1_copy(d).wait_send()
+        loss_3_copy(d).wait_send()
 
     each(1, X, sent_ring)
     for d in (1, 2, 6, 7):
@@ -531,7 +538,8 @@
     each(1, X, lambda d: grad_x(d).wait_send())
     each(1, X, lambda d: grad_y(d).wait_send())
     each(1, XY, lambda d: loss_2_copy(d).wait_recv())
-    total = jnp.sum(jnp.sum(loss_2[...], axis=0), axis=0, keepdims=True)
+    each(1, ZC, lambda d: loss_3_copy(d).wait_recv())
+    total = jnp.sum(jnp.sum(loss_2[...], axis=0) + jnp.sum(loss_3[...], axis=0), axis=0, keepdims=True)
     loss_ref[...] = jnp.sum(total, axis=1, keepdims=True) * (1.0 / (2 * XY * BLOCK))
     store_loss = pltpu.make_async_copy(loss_ref, loss_out, store_sem.at[2])
     store_loss.start()
@@ -595,6 +603,7 @@
             pltpu.VMEM((XY, 4, 128), f32),
             pltpu.VMEM((ZC, 4, 128), f32),
             pltpu.VMEM((XY, 4, 128), f32),
+            pltpu.VMEM((ZC, 4, 128), f32),
             pltpu.VMEM((SIDE, emb), bf16),
             pltpu.VMEM((SIDE, emb), bf16),
             pltpu.VMEM((SIDE, emb), bf16),
@@ -616,7 +625,7 @@
             dma(X), dma(X), dma(X), dma(X), dma(X), dma(X),
             dma(Z), dma(Z), dma(2), dma(2), dma(Z), dma(Z), dma(X), dma(X), dma(Y), dma(Y),
             dma(XY), dma(XY), dma(XY), dma(XY),
-            dma(ZC), dma(ZC), dma(XY), dma(XY), dma(ZC), dma(ZC), dma(XY), dma(XY),
+            dma(ZC), dma(ZC), dma(XY), dma(XY), dma(ZC), dma(ZC), dma(XY), dma(XY), dma(ZC), dma(ZC),
             pltpu.SemaphoreType.DMA, pltpu.SemaphoreType.DMA,
             dma(2), dma(2), dma(2), dma(2), dma(2), dma(2), dma(2), dma(2),
             dma(X), dma(X), dma(Y), dma(Y), dma(Y), dma(Y), dma(X), dma(X),

time: 61 us -> 61.4 us (level)
  no operation moved by 1% of the time
where the time goes in v8:
time: 61.4 us; the launch traced here: 61.2 us
  Pallas kernels  56.5 us (92%)
  between operations  3.05 us (5%)
  local copies, waits for them, and re-layouts  1.67 us (3%)
    pallas_call x1, Pallas kernels, body(): pl.pallas_call(kernel, out_shape=(jax.ShapeDtypeStruct((1, ROWS, emb), f3...  56.5 us
    unnamed x1, local copies, waits for them, and re-layouts  1.67 us

profile of v8, /device:TPU:1, one launch (start us, length us, event | category | flops | bytes accessed | tf_op | source)
XLA Modules:
  0.0 61.2 jit_solution(10490655344677842979)
XLA Ops:
  1.3 56.5 %contrastive.1 = (f32[1,64,1024]{2,1,0:T(8,128)}, f32[1,1]{1,0:T(1,128)}) custom-call(bf16[256,1536]{1,0:T(8,128)(2,1)} %feat_i.1, bf16[256,256]{1,0:T(8,128)(2,1)} %feat_t.1, f32[12,128]{1,0:T(8,128)} %bitcast.7, f32[2,128]{1,0:T(2,128)} %bitcast.8, bf16[1536,1024]{1,0:T(8,128)(2,1)} %proj_i.1, bf16[256,1024]{1,0:T(8,128)(2,1)} %proj_t.1, ...), custom_call_target="tpu_custom_call" | custom-call | tf_op jit(solution)/shard_map/contrastive/pallas_call | solution.py:569
  57.8 1.7 %copy.13 = f32[1,64,1024]{2,1,0:T(8,128)} copy(f32[1,64,1024]{2,1,0:T(8,128)} %get-tuple-element.8) | data formatting | bytes 524288
